TPU v7x, 128 devices: a whole 4x4x4 slice. The times are simulated.
128 devices in a mesh: dp: 4 (over x_lo, core), tp: 32 (over y, x_hi, z).
Axes of the slice: x: 4 (x_hi: 2, x_lo: 2; x = x_hi * 2 + x_lo), y: 4, z: 4, core: 2. Of those that a mesh axis runs over, the one named last changes fastest.
Arguments:
- layer_inputs: bfloat16 [2, 1536, 4608], P(None, 'dp'), may hold values from -120 to 120
- out_grad: bfloat16 [1536, 4608], P('dp'), may hold values from -6 to 6
- gain: float32 [2, 4608], replicated, may hold values from 0.5 to 1.5
- w_query: bfloat16 [2, 4608, 4096], P(None, None, 'tp'), may hold values from -0.09375 to 0.09375
- w_key: bfloat16 [2, 4608, 2048], P(None, None, 'tp'), may hold values from -0.09375 to 0.09375
- w_value: bfloat16 [2, 4608, 2048], P(None, None, 'tp'), may hold values from -0.09375 to 0.09375
- w_out: bfloat16 [2, 4096, 4608], P(None, 'tp'), may hold values from -0.09375 to 0.09375
- doc_lengths: int32 [4, 4], P('dp'), may hold values from 1 to 192, 384 in all within a row
- window_reach: int32 [2], replicated, may hold values from 48 to 384, as said below
Outputs:
- input_grad: bfloat16 [1536, 4608], P('dp')
- grad_w_query: float32 [2, 4608, 4096], P(None, 'dp', 'tp')
- grad_w_key: float32 [2, 4608, 2048], P(None, 'dp', 'tp')
- grad_w_value: float32 [2, 4608, 2048], P(None, 'dp', 'tp')
- grad_w_out: float32 [2, 4096, 4608], P(None, 'tp', 'dp')
- grad_gain: float32 [2, 4608], replicated
Inputs may be any that keep to these rules, and one draw needn't show every extreme that they name: `doc_lengths`: the 4 lengths of a row fill its sequence's 384 positions in order; in every row the longest document has exactly 192 positions. `window_reach`: exactly one sublayer has reach 384 (it sees all earlier positions of its document); the other's reach is at most 192.
All inputs are finite; a program needn't handle non-finite values.
Results may differ from a plain program's by a relative error of at most 0.025.
Values may be sent and summed in bfloat16 or wider, within the bound.
A program may use at most 128 MiB of HBM per device.

v0:
```python
import functools
import math

import jax
import jax.numpy as jnp
from jax import lax
from jax.sharding import Mesh
from jax.sharding import PartitionSpec as P

D = 4608
HEADS = 32
HD = 128
SEQ_LEN = 384
LAYERS = 2
TP = ("tp_0", "tp_1", "tp_2")
DP = ("dp_0", "dp_1")
DP_TP = ("dp_0", "dp_1", "tp_0", "tp_1", "tp_2")


softcap = 50.0
epsilon = 1e-06


def swapped(x, axis, bit):
    return lax.ppermute(x, axis, [(i, i ^ 1 << bit) for i in range(lax.axis_size(axis))])


def sum_in_order(pieces, axes, turns):
    inside = pieces.shape[1:]
    pieces = pieces.reshape(*(lax.axis_size(a) for a in axes), *inside)
    pieces = jnp.moveaxis(pieces, turns, range(len(axes))).reshape(-1, *inside)
    for k in turns:
        pieces = lax.psum_scatter(pieces, axes[k], scatter_dimension=0, tiled=True)
    return pieces[0]


def split_up(x, dim, peers):
    before, after = (x.shape[:dim], x.shape[dim + 1 :])
    return jnp.moveaxis(x.reshape(*before, peers, -1, *after), dim, 0)


def summed_rows(x, axes, turns, dim):
    peers = lax.axis_size(axes)
    return sum_in_order(split_up(x, dim, peers), axes, turns)


def sum_at_owner(x, axis, dim):
    pieces = split_up(x, dim, lax.axis_size(axis))
    arrived = lax.all_to_all(pieces, axis, split_axis=0, concat_axis=0, tiled=True)
    return arrived.astype(jnp.float32).sum(axis=0)


def in_one_piece(arrays, axis, dim, along):
    widths = [a.shape[along] for a in arrays]
    both = jnp.concatenate(arrays, axis=along)
    out = sum_at_owner(both, axis, dim)
    return tuple(jnp.split(out, [sum(widths[:k]) for k in range(1, len(widths))], axis=along))


def by_axis(x, axes):
    return functools.reduce(lax.psum, axes, x)


def rope_tables(length, head_width):
    half_width = head_width // 2
    frequencies = jnp.exp(
        -jnp.arange(half_width).astype(jnp.float32) * (2.0 * math.log(10000.0) / head_width)
    )
    angles = jnp.arange(length).astype(jnp.float32)[:, None] * frequencies[None, :]
    return (jnp.cos(angles)[:, None, :], jnp.sin(angles)[:, None, :])


def rotate(values, cosine, sine_table):
    half_width = values.shape[-1] // 2
    first_half = values[..., :half_width]
    second_half = values[..., half_width:]
    return jnp.concatenate(
        [
            first_half * cosine - second_half * sine_table,
            second_half * cosine + first_half * sine_table,
        ],
        axis=-1,
    )


def unrotate(values, cosine, sine_table):
    half_width = values.shape[-1] // 2
    first_half = values[..., :half_width]
    second_half = values[..., half_width:]
    return jnp.concatenate(
        [
            first_half * cosine + second_half * sine_table,
            second_half * cosine - first_half * sine_table,
        ],
        axis=-1,
    )


def allowed_pairs(lengths_row, reach, length):
    doc_ends = jnp.cumsum(lengths_row)
    places = jnp.arange(length, dtype=jnp.int32)
    document = jnp.sum((places[:, None] >= doc_ends[None, :]).astype(jnp.int32), axis=1)
    same_doc = document[:, None] == document[None, :]
    causal = places[None, :] <= places[:, None]
    in_window = places[:, None] - places[None, :] < reach
    return same_doc & causal & in_window


def join_halves(own_part, other_part, parity):
    return jnp.where(
        parity == 0,
        jnp.concatenate([own_part, other_part], axis=-1),
        jnp.concatenate([other_part, own_part], axis=-1),
    )


def split_halves(matrix, parity):
    half_width = matrix.shape[-1] // 2
    lower_part = matrix[..., :half_width]
    upper_part = matrix[..., half_width:]
    return (
        jnp.where(parity == 0, lower_part, upper_part),
        jnp.where(parity == 0, upper_part, lower_part),
    )


def contract_rows(left_side, right_side):
    return lax.dot_general(
        left_side, right_side, (((0,), (0,)), ((), ())), preferred_element_type=jnp.float32
    )


def contract_cols(left_side, right_side):
    return lax.dot_general(
        left_side, right_side, (((1,), (1,)), ((), ())), preferred_element_type=jnp.float32
    )


def norm_backward(inputs, grad_normed, upstream, gain_row):
    matrix_rows = inputs.astype(jnp.float32)
    reciprocal = lax.rsqrt(jnp.mean(matrix_rows * matrix_rows, axis=-1, keepdims=True) + epsilon)
    unit_rows = matrix_rows * reciprocal
    scaled_grad = grad_normed * gain_row
    branch = reciprocal * (
        scaled_grad - unit_rows * jnp.mean(scaled_grad * unit_rows, axis=-1, keepdims=True)
    )
    layer_grad = (upstream.astype(jnp.float32) + branch).astype(jnp.bfloat16)
    return (layer_grad, grad_normed * unit_rows)


def local(layer_inputs, out_grad, gain, w_query, w_key, w_value, w_out, doc_lengths, window_reach):
    device_rank = lax.axis_index(TP)
    parity = device_rank % 2
    local_rows = SEQ_LEN // lax.axis_size(TP)
    query_heads = w_query.shape[2] // HD
    score_scale = (D // HEADS) ** (-0.5)
    cosine_table, sine_table = rope_tables(SEQ_LEN, HD)
    first_own = device_rank * local_rows
    full_upstream = out_grad
    grads_by_layer = [None] * LAYERS
    gain_terms = [None] * LAYERS
    for layer_number in reversed(range(LAYERS)):
        whole_inputs = layer_inputs[layer_number]
        gain_row = gain[layer_number]
        query_weight = w_query[layer_number]
        key_weight = w_key[layer_number]
        value_weight = w_value[layer_number]
        out_weight = w_out[layer_number]
        matrix_rows = whole_inputs.astype(jnp.float32)
        reciprocal = lax.rsqrt(
            jnp.mean(matrix_rows * matrix_rows, axis=-1, keepdims=True) + epsilon
        )
        normed = (matrix_rows * reciprocal * gain_row).astype(jnp.bfloat16)
        queries = rotate(
            jnp.dot(normed, query_weight, preferred_element_type=jnp.float32).reshape(
                SEQ_LEN, query_heads, HD
            ),
            cosine_table,
            sine_table,
        ).astype(jnp.bfloat16)
        own_key = jnp.dot(normed, key_weight, preferred_element_type=jnp.float32)
        own_value = jnp.dot(normed, value_weight, preferred_element_type=jnp.float32)
        partner_key, partner_value = swapped((own_key, own_value), TP, 0)
        key_raw = join_halves(own_key, partner_key, parity)
        value_raw = join_halves(own_value, partner_value, parity)
        key_heads = 1
        keys_rope = rotate(
            key_raw.reshape(SEQ_LEN, key_heads, HD), cosine_table, sine_table
        ).astype(jnp.bfloat16)
        values_cast = value_raw.reshape(SEQ_LEN, key_heads, HD).astype(jnp.bfloat16)
        keys_shared = jnp.repeat(keys_rope, query_heads // key_heads, axis=1)
        values_shared = jnp.repeat(values_cast, query_heads // key_heads, axis=1)
        allowed = allowed_pairs(doc_lengths[0], window_reach[layer_number], SEQ_LEN)
        scores = (
            jnp.einsum("thd,shd->hts", queries, keys_shared, preferred_element_type=jnp.float32)
            * score_scale
        )
        squashed = jnp.tanh(scores / softcap)
        raised = jnp.where(allowed[None], jnp.exp(softcap * squashed), 0.0)
        probability = raised / jnp.sum(raised, axis=-1, keepdims=True)
        rounded_prob = probability.astype(jnp.bfloat16)
        attended = jnp.einsum(
            "hts,shd->thd", rounded_prob, values_shared, preferred_element_type=jnp.float32
        ).astype(jnp.bfloat16)
        attended_flat = attended.reshape(SEQ_LEN, query_heads * HD)
        grad_attended = contract_cols(full_upstream, out_weight).astype(jnp.bfloat16)
        grad_w_out = contract_rows(attended_flat, full_upstream)
        grad_heads = grad_attended.reshape(SEQ_LEN, query_heads, HD)
        row_delta = jnp.sum(
            grad_heads.astype(jnp.float32) * attended.astype(jnp.float32), axis=-1
        ).T
        grad_probs = jnp.einsum(
            "thd,shd->hts", grad_heads, values_shared, preferred_element_type=jnp.float32
        )
        grad_scores = (
            probability
            * (grad_probs - row_delta[:, :, None])
            * (1.0 - squashed * squashed)
            * score_scale
        ).astype(jnp.bfloat16)
        grad_queries = (
            unrotate(
                jnp.einsum(
                    "hts,shd->thd", grad_scores, keys_shared, preferred_element_type=jnp.float32
                ),
                cosine_table,
                sine_table,
            )
            .astype(jnp.bfloat16)
            .reshape(SEQ_LEN, query_heads * HD)
        )
        key_each = unrotate(
            jnp.einsum("hts,thd->shd", grad_scores, queries, preferred_element_type=jnp.float32),
            cosine_table,
            sine_table,
        ).astype(jnp.bfloat16)
        value_each = jnp.einsum(
            "hts,thd->shd", rounded_prob, grad_heads, preferred_element_type=jnp.float32
        ).astype(jnp.bfloat16)
        grad_w_query = contract_rows(normed, grad_queries)
        own_key_grad = key_each[:, 0, :]
        own_value_grad = value_each[:, 0, :]
        kept_key, sent_key = split_halves(own_key_grad, parity)
        kept_value, sent_value = split_halves(own_value_grad, parity)
        partner_key_grad, partner_value_grad = swapped((sent_key, sent_value), TP, 0)
        grad_w_key = contract_rows(normed, kept_key) + contract_rows(normed, partner_key_grad)
        grad_w_value = contract_rows(normed, kept_value) + contract_rows(normed, partner_value_grad)
        pair_terms = (
            (jnp.stack([kept_key, partner_key_grad]), key_weight),
            (jnp.stack([kept_value, partner_value_grad]), value_weight),
        )
        totals = contract_cols(grad_queries, query_weight)
        for stacked, weight in pair_terms:
            for grad_member in range(stacked.shape[0]):
                totals = totals + contract_cols(stacked[grad_member], weight)
        local_grad = summed_rows(totals.astype(jnp.bfloat16), TP, (0, 2, 1), 0).astype(jnp.float32)
        own_inputs = lax.dynamic_slice_in_dim(whole_inputs, first_own, local_rows, 0)
        own_upstream = lax.dynamic_slice_in_dim(full_upstream, first_own, local_rows, 0)
        local_layer, gain_rows = norm_backward(own_inputs, local_grad, own_upstream, gain_row)
        gain_terms[layer_number] = jnp.sum(gain_rows, axis=0)
        full_upstream = lax.all_gather(local_layer, TP, axis=0, tiled=True)
        layer_grads = (grad_w_query, grad_w_key, grad_w_value, grad_w_out)
        layer_grads = (
            *in_one_piece(
                (
                    grad_w_query.astype(jnp.bfloat16),
                    grad_w_key.astype(jnp.bfloat16),
                    grad_w_value.astype(jnp.bfloat16),
                ),
                DP,
                0,
                1,
            ),
            sum_at_owner(grad_w_out.astype(jnp.bfloat16), DP, 1),
        )
        grads_by_layer[layer_number] = layer_grads
    stacks = [
        jnp.stack([grads_by_layer[layer_number][member] for layer_number in range(LAYERS)])
        for member in range(4)
    ]
    group_count = lax.axis_size(DP)
    gain_total = by_axis(jnp.stack(gain_terms), DP_TP)
    return (
        full_upstream,
        stacks[0] / group_count,
        stacks[1] / group_count,
        stacks[2] / group_count,
        stacks[3] / group_count,
        gain_total / group_count,
    )


def solution(mesh):
    split = Mesh(mesh.devices.reshape(2, 2, 4, 2, 4), ("dp_0", "dp_1", "tp_0", "tp_1", "tp_2"))
    in_specs = (
        P(None, DP, None),
        P(DP, None),
        P(),
        P(None, None, TP),
        P(None, None, TP),
        P(None, None, TP),
        P(None, TP, None),
        P(DP, None),
        P(),
    )
    out_specs = (
        P(DP, None),
        P(None, DP, TP),
        P(None, DP, TP),
        P(None, DP, TP),
        P(None, TP, DP),
        P(),
    )
    return jax.shard_map(local, mesh=split, in_specs=in_specs, out_specs=out_specs, check_vma=False)
```

profile of v0, /device:TPU:0, one launch (start us, length us, event | category | flops | bytes accessed | tf_op | source)
XLA Modules:
  0.0 564.1 jit_solution(18148293179558734364)
XLA Ops:
  8.2 4.0 fusion.11
  13.3 2.5 fusion.73
  22.8 3.8 fusion.48
  26.7 3.4 fusion.51
  32.0 2.3 fusion.224
  35.1 2.3 fusion.120
  50.8 2.9 reshape_reshape.6
  53.7 2.6 copy.55
  56.4 3.7 copy.61
  60.2 43.5 %reduce-scatter.17.cloned.1.call-done = bf16[8,55296]{1,0:T(8,128)(2,1)} async-done(((bf16[32,55296]{1,0:T(8,128)(2,1)}), bf16[8,55296]{1,0:T(8,128)(2,1)}) %reduce-scatter.17.cloned.1.call-update) | async-done | bytes 884752
  105.0 46.0 %all-reduce.3.cloned.1.call-done = bf16[8,12,4608]{2,0,1:T(8,128)(2,1)} async-done(((bf16[8,12,4608]{2,0,1:T(8,128)(2,1)}), bf16[8,12,4608]{2,0,1:T(8,128)(2,1)}) %all-reduce.3.cloned.1.call-update) | async-done | bytes 884752
  153.3 6.5 %fusion.249 = (bf16[1,384,4608]{2,1,0:T(8,128)(2,1)}, bf16[1,384,4608]{2,1,0:T(8,128)(2,1)}) fusion(bf16[2,384,4608]{2,1,0:T(8,128)(2,1)} %param.9), kind=kLoop, calls=%fused_computation.318 | loop fusion | bytes 14155776 | tf_op jit(solution)/shard_map/slice | solution.py:163
  160.9 10.0 %reduce-scatter.9.cloned.1.call-done = bf16[1,12,4608]{2,1,0:T(8,128)(2,1)} async-done(((bf16[2,12,4608]{2,1,0:T(8,128)(2,1)}), bf16[1,12,4608]{2,1,0:T(8,128)(2,1)}) %reduce-scatter.9.cloned.1.call-update) | async-done | bytes 110608 | tf_op jit(solution)/shard_map/reduce_scatter | solution.py:33
  174.7 3.3 fusion.69
  179.9 2.5 collective-permute-done.5
  183.3 73.8 %all-gather.5.cloned.1.call-done = bf16[32,12,4608]{2,1,0:T(8,128)(2,1)} async-done(((bf16[1,12,4608]{2,1,0:T(8,128)(2,1)}), bf16[32,12,4608]{2,1,0:T(8,128)(2,1)}) %all-gather.5.cloned.1.call-update) | async-done | bytes 3538960 | tf_op jit(solution)/shard_map/all_gather | solution.py:261
  257.1 4.1 reshape.705
  261.3 2.5 fusion.123
  274.4 2.9 fusion.17
  277.3 5.8 %reshape_reshape.7 = bf16[4,2,4,12,4608]{4,3,2,1,0:T(8,128)(2,1)} reshape(bf16[384,4608]{1,0:T(8,128)(2,1)} %fusion.17) | data formatting | bytes 7077888 | tf_op jit(solution)/shard_map/reshape;reshape | solution.py:30
  283.1 4.9 copy.43
  289.2 2.8 convolution_convert_fusion.2
  293.3 4.3 all-to-all-start.3
  297.9 4.3 fusion.212
  302.3 3.4 fusion.196
  305.7 4.5 convolution_convert_fusion
  312.4 25.7 %reduce-scatter.11.cloned.1.call-done = bf16[8,12,4608]{2,1,0:T(8,128)(2,1)} async-done(((bf16[32,12,4608]{2,1,0:T(8,128)(2,1)}), bf16[8,12,4608]{2,1,0:T(8,128)(2,1)}) %reduce-scatter.11.cloned.1.call-update) | async-done | bytes 884752 | tf_op jit(solution)/shard_map/reduce_scatter | solution.py:33
  338.2 3.8 fusion.21
  344.8 2.2 fusion.211
  347.0 2.2 fusion.193
  349.2 15.3 %reduce-scatter.13.cloned.1.call-done = bf16[2,12,4608]{2,1,0:T(8,128)(2,1)} async-done(((bf16[8,12,4608]{2,1,0:T(8,128)(2,1)}), bf16[2,12,4608]{2,1,0:T(8,128)(2,1)}) %reduce-scatter.13.cloned.1.call-update) | async-done | bytes 221200 | tf_op jit(solution)/shard_map/reduce_scatter | solution.py:33
  367.4 4.4 convolution_convert_fusion.1
  371.8 10.9 %reduce-scatter.15.cloned.1.call-done = bf16[1,12,4608]{2,1,0:T(8,128)(2,1)} async-done(((bf16[2,12,4608]{2,1,0:T(8,128)(2,1)}), bf16[1,12,4608]{2,1,0:T(8,128)(2,1)}) %reduce-scatter.15.cloned.1.call-update) | async-done | bytes 110608 | tf_op jit(solution)/shard_map/reduce_scatter | solution.py:33
  384.5 4.5 all-to-all-start.1
  390.9 3.6 fusion.18
  394.6 24.0 %all-to-all-done.1 = bf16[4,1152,256]{1,2,0:T(8,128)(2,1)} async-done(((bf16[4,1152,256]{1,2,0:T(8,128)(2,1)}), bf16[4,1152,256]{1,2,0:T(8,128)(2,1)}, u32[]{:S(2)}, u32[]{:S(2)}) %all-to-all-start.1) | async-done | bytes 2359328 | tf_op jit(solution)/shard_map/all_to_all | solution.py:49
  418.6 3.8 all-to-all-start.2
  422.4 3.7 fusion.19
  427.9 14.5 %all-to-all-done.2 = bf16[4,128,1152]{2,1,0:T(8,128)(2,1)S(1)} async-done(((bf16[4,128,1152]{2,1,0:T(8,128)(2,1)}), bf16[4,128,1152]{2,1,0:T(8,128)(2,1)S(1)}, u32[]{:S(2)}, u32[]{:S(2)}) %all-to-all-start.2) | async-done | bytes 1179680 | tf_op jit(solution)/shard_map/all_to_all | solution.py:49
  442.4 3.6 all-to-all-start
  447.5 2.2 convert_reduce_fusion
  453.3 38.0 %all-to-all-done = bf16[4,1152,256]{1,2,0:T(8,128)(2,1)S(1)} async-done(((bf16[4,1152,256]{1,2,0:T(8,128)(2,1)}), bf16[4,1152,256]{1,2,0:T(8,128)(2,1)S(1)}, u32[]{:S(2)}, u32[]{:S(2)}) %all-to-all-start) | async-done | bytes 2359328 | tf_op jit(solution)/shard_map/all_to_all | solution.py:49
  495.5 7.4 %psum.35 = f32[2,4608]{1,0:T(2,128)S(1)} all-reduce(f32[2,4608]{1,0:T(2,128)S(1)} %pad_maximum_fusion.20), channel_id=1, replica_groups=mesh['dp_0'=2,'dp_1'=2,'tp_0'=4,'tp_1'=2,'tp_2'=4] {'dp_0'}, use_global_device_ids=true, to_apply=%region_24.25 | all-reduce | flops 9216 | bytes 73728 | tf_op jit(solution)/shard_map/psum | solution.py:61
  502.9 3.5 psum.36
  506.4 17.3 %psum.37 = f32[2,4608]{1,0:T(2,128)S(1)} all-reduce(f32[2,4608]{1,0:T(2,128)S(1)} %psum.36), channel_id=1, replica_groups=mesh['dp_0'=2,'dp_1'=2,'tp_0'=4,'tp_1'=2,'tp_2'=4] {'tp_0'}, use_global_device_ids=true, to_apply=%region_26.27 | all-reduce | flops 9216 | bytes 73728 | tf_op jit(solution)/shard_map/psum | solution.py:61
  523.7 9.0 %psum.38 = f32[2,4608]{1,0:T(2,128)S(1)} all-reduce(f32[2,4608]{1,0:T(2,128)S(1)} %psum.37), channel_id=1, replica_groups=mesh['dp_0'=2,'dp_1'=2,'tp_0'=4,'tp_1'=2,'tp_2'=4] {'tp_1'}, use_global_device_ids=true, to_apply=%region_27.28 | all-reduce | flops 9216 | bytes 73728 | tf_op jit(solution)/shard_map/psum | solution.py:61
  532.7 17.5 %psum.39 = f32[2,4608]{1,0:T(2,128)S(1)} all-reduce(f32[2,4608]{1,0:T(2,128)S(1)} %psum.38), channel_id=1, replica_groups=mesh['dp_0'=2,'dp_1'=2,'tp_0'=4,'tp_1'=2,'tp_2'=4] {'tp_2'}, use_global_device_ids=true, to_apply=%region_28.29 | all-reduce | flops 9216 | bytes 73728 | tf_op jit(solution)/shard_map/psum | solution.py:61
  550.9 5.9 %reshape.707 = bf16[384,4608]{1,0:T(8,128)(2,1)} reshape(bf16[32,12,4608]{2,1,0:T(8,128)(2,1)} %all-gather.7.cloned.1.call-done) | data formatting | bytes 7077888
  (275 shorter events, 71.3 us)
Async XLA Ops:
  7.2 96.5 %reduce-scatter.17.cloned.1.call-start = ((), (), s32[]{:S(2)}) async-start(), calls=%async_computation.15 | async-start | bytes 4423680
  8.2 14.7 %copy-start.52 = (f32[4608]{0:T(1024)}, f32[4608]{0:T(1024)S(1)}, u32[]{:S(2)}) copy-start(f32[4608]{0:T(1024)S(1)} %get-tuple-element.43) | copy-start | bytes 55300
  8.2 18.5 %copy-start.47 = (f32[4608]{0:T(1024)}, f32[4608]{0:T(1024)S(1)}, u32[]{:S(2)}) copy-start(f32[4608]{0:T(1024)S(1)} %get-tuple-element.42) | copy-start | bytes 55300
  8.2 5.1 copy-start
  12.2 14.5 %copy-start.65 = (f32[384]{0:T(512)}, f32[384]{0:T(512)S(1)}, u32[]{:S(2)}) copy-start(f32[384]{0:T(512)S(1)} %add_rsqrt_fusion) | copy-start | bytes 4612
  15.8 15.2 %collective-permute-start.4 = (f32[384,64]{0,1:T(8,128)S(1)}, f32[384,64]{0,1:T(8,128)S(1)}, u32[]{:S(2)}, u32[]{:S(2)}) collective-permute-start(f32[384,64]{0,1:T(8,128)S(1)} %fusion.73), channel_id=1, source_target_pairs={{0,1},{1,0},{2,3},{3,2},{4,5},{5,4},{6,7},{7,6},{8,9},{9,8},{10,11... | collective-permute-start | bytes 294920 | tf_op jit(solution)/shard_map/ppermute | solution.py:25
  17.9 4.9 copy-start.68
  19.3 11.8 %collective-permute-start = (f32[384,64]{0,1:T(8,128)S(1)}, f32[384,64]{0,1:T(8,128)S(1)}, u32[]{:S(2)}, u32[]{:S(2)}) collective-permute-start(f32[384,64]{0,1:T(8,128)S(1)} %fusion.82), channel_id=1, source_target_pairs={{0,1},{1,0},{2,3},{3,2},{4,5},{5,4},{6,7},{7,6},{8,9},{9,8},{10,11... | collective-permute-start | bytes 294920 | tf_op jit(solution)/shard_map/ppermute | solution.py:25
  20.8 16.7 %collective-permute-start.1 = (bf16[384,64]{0,1:T(8,128)(2,1)S(1)}, bf16[384,64]{0,1:T(8,128)(2,1)S(1)}, u32[]{:S(2)}, u32[]{:S(2)}) collective-permute-start(bf16[384,64]{0,1:T(8,128)(2,1)S(1)} %fusion.78), channel_id=1, source_target_pairs={{0,1},{1,0},{2,3},{3,2},{4,5},{5,4},{6,7},{7,6},{8,9},{9,8},{10,11... | collective-permute-start | bytes 147464 | tf_op jit(solution)/shard_map/ppermute | solution.py:25
  31.1 6.6 %copy-start.7 = (bf16[384,4608]{1,0:T(8,128)(2,1)S(1)}, bf16[384,4608]{1,0:T(8,128)(2,1)}, u32[]{:S(2)}) copy-start(bf16[384,4608]{1,0:T(8,128)(2,1)} %param.10) | copy-start | bytes 10616836
  31.1 6.5 %copy-start.71 = (bf16[2,128,4608]{2,1,0:T(8,128)(2,1)S(1)}, bf16[2,128,4608]{2,1,0:T(8,128)(2,1)}, u32[]{:S(2)}) copy-start(bf16[2,128,4608]{2,1,0:T(8,128)(2,1)} %param.15) | copy-start | bytes 7077892
  31.6 7.2 %copy-start.31 = (bf16[384,64]{0,1:T(8,128)(2,1)}, bf16[384,64]{0,1:T(8,128)(2,1)S(1)}, u32[]{:S(2)}) copy-start(bf16[384,64]{0,1:T(8,128)(2,1)S(1)} %get-tuple-element.70) | copy-start | bytes 147460
  31.6 7.2 %copy-start.33 = (bf16[384,64]{0,1:T(8,128)(2,1)}, bf16[384,64]{0,1:T(8,128)(2,1)S(1)}, u32[]{:S(2)}) copy-start(bf16[384,64]{0,1:T(8,128)(2,1)S(1)} %get-tuple-element.71) | copy-start | bytes 147460
  31.7 7.2 %copy-start.35 = (bf16[384,64]{0,1:T(8,128)(2,1)}, bf16[384,64]{0,1:T(8,128)(2,1)S(1)}, u32[]{:S(2)}) copy-start(bf16[384,64]{0,1:T(8,128)(2,1)S(1)} %get-tuple-element.72) | copy-start | bytes 147460
  31.7 7.2 %copy-start.37 = (bf16[384,64]{0,1:T(8,128)(2,1)}, bf16[384,64]{0,1:T(8,128)(2,1)S(1)}, u32[]{:S(2)}) copy-start(bf16[384,64]{0,1:T(8,128)(2,1)S(1)} %get-tuple-element.73) | copy-start | bytes 147460
  38.9 5.6 copy-start.9
  40.9 5.9 %copy-start.17 = (bf16[384,128]{0,1:T(8,128)(2,1)}, bf16[384,128]{0,1:T(8,128)(2,1)S(1)}, u32[]{:S(2)}) copy-start(bf16[384,128]{0,1:T(8,128)(2,1)S(1)} %fusion.60) | copy-start | bytes 294916
  41.8 6.1 %collective-permute-start.2 = (bf16[384,64]{0,1:T(8,128)(2,1)S(1)}, bf16[384,64]{0,1:T(8,128)(2,1)S(1)}, u32[]{:S(2)}, u32[]{:S(2)}) collective-permute-start(bf16[384,64]{0,1:T(8,128)(2,1)S(1)} %get-tuple-element.49), channel_id=1, source_target_pairs={{0,1},{1,0},{2,3},{3,2},{4,5},{5,4},{6,7},{7,6},{8,9},{9,8},{10,11... | collective-permute-start | bytes 147464 | tf_op jit(solution)/shard_map/ppermute | solution.py:25
  42.4 6.6 %collective-permute-start.3 = (bf16[384,64]{0,1:T(8,128)(2,1)S(1)}, bf16[384,64]{0,1:T(8,128)(2,1)S(1)}, u32[]{:S(2)}, u32[]{:S(2)}) collective-permute-start(bf16[384,64]{0,1:T(8,128)(2,1)S(1)} %broadcast_select_fusion.2), channel_id=1, source_target_pairs={{0,1},{1,0},{2,3},{3,2},{4,5},{5,4},{6,7},{7,6},{8,9},{9,8},{10,11... | collective-permute-start | bytes 147464 | tf_op jit(solution)/shard_map/ppermute | solution.py:25
  60.1 43.7 %copy-start.77 = (u32[128]{0:T(128)S(1)}, u32[128]{0:T(128)}, u32[]{:S(2)}) copy-start(u32[128]{0:T(128)} %constant.80) | copy-start | bytes 1540
  60.1 90.9 %all-reduce.3.cloned.1.call-start = ((), (), s32[]{:S(2)}) async-start(), calls=%async_computation.16 | async-start | bytes 1769472
  103.7 67.1 %reduce-scatter.9.cloned.1.call-start = ((), (), s32[]{:S(2)}) async-start(), calls=%async_computation.9 | async-start | bytes 442368 | tf_op jit(solution)/shard_map/reduce_scatter | solution.py:33
  153.2 17.7 %copy-start.53 = (f32[4608]{0:T(1024)S(1)}, f32[4608]{0:T(1024)}, u32[]{:S(2)}) copy-start(f32[4608]{0:T(1024)} %copy-done.52) | copy-start | bytes 55300
  153.2 21.5 %copy-start.5 = (bf16[2,4608,64]{1,2,0:T(8,128)(2,1)S(1)}, bf16[2,4608,64]{1,2,0:T(8,128)(2,1)}, u32[]{:S(2)}) copy-start(bf16[2,4608,64]{1,2,0:T(8,128)(2,1)} %param.14) | copy-start | bytes 3538948
  153.2 21.5 %copy-start.48 = (f32[4608]{0:T(1024)S(1)}, f32[4608]{0:T(1024)}, u32[]{:S(2)}) copy-start(f32[4608]{0:T(1024)} %copy-done.47) | copy-start | bytes 55300
  153.2 21.5 %copy-start.66 = (f32[384]{0:T(512)S(1)}, f32[384]{0:T(512)}, u32[]{:S(2)}) copy-start(f32[384]{0:T(512)} %copy-done.65) | copy-start | bytes 4612
  153.2 103.9 %all-gather.5.cloned.1.call-start = ((), (), s32[]{:S(2)}) async-start(), calls=%async_computation.13 | async-start | bytes 4866048 | tf_op jit(solution)/shard_map/all_gather | solution.py:261
  174.6 7.8 %copy-start.13 = (bf16[384,384]{0,1:T(8,128)(2,1)S(1)}, bf16[384,384]{0,1:T(8,128)(2,1)}, u32[]{:S(2)}) copy-start(bf16[384,384]{0,1:T(8,128)(2,1)} %get-tuple-element.76) | copy-start | bytes 884740
  174.6 163.5 %reduce-scatter.11.cloned.1.call-start = ((), (), s32[]{:S(2)}) async-start(), calls=%async_computation.10 | async-start | bytes 5898240 | tf_op jit(solution)/shard_map/reduce_scatter | solution.py:33
  178.0 5.2 copy-start.72
  178.1 4.3 collective-permute-start.5
  263.9 5.2 copy-start.10
  265.9 5.6 copy-start.18
  266.8 5.9 %collective-permute-start.6 = (bf16[384,64]{0,1:T(8,128)(2,1)S(1)}, bf16[384,64]{0,1:T(8,128)(2,1)S(1)}, u32[]{:S(2)}, u32[]{:S(2)}) collective-permute-start(bf16[384,64]{0,1:T(8,128)(2,1)S(1)} %get-tuple-element.46), channel_id=1, source_target_pairs={{0,1},{1,0},{2,3},{3,2},{4,5},{5,4},{6,7},{7,6},{8,9},{9,8},{10,11... | collective-permute-start | bytes 147464 | tf_op jit(solution)/shard_map/ppermute | solution.py:25
  268.5 5.3 collective-permute-start.7
  292.0 5.8 %copy-start.69 = (f32[384]{0:T(512)S(1)}, f32[384]{0:T(512)}, u32[]{:S(2)}) copy-start(f32[384]{0:T(512)} %copy-done.68) | copy-start | bytes 4612
  293.3 91.2 %all-to-all-start.3 = ((bf16[4,128,1152]{2,1,0:T(8,128)(2,1)}), bf16[4,128,1152]{2,1,0:T(8,128)(2,1)}, u32[]{:S(2)}, u32[]{:S(2)}) async-start(bf16[4,128,1152]{2,1,0:T(8,128)(2,1)} %bitcast.307), calls=%async_computation.7 | async-start | bytes 2359296 | tf_op jit(solution)/shard_map/all_to_all | solution.py:49
  297.6 66.9 %reduce-scatter.13.cloned.1.call-start = ((), (), s32[]{:S(2)}) async-start(), calls=%async_computation.11 | async-start | bytes 1474560 | tf_op jit(solution)/shard_map/reduce_scatter | solution.py:33
  302.3 8.0 %slice-start = ((s8[7077888]{0:T(1024)(128)(4,1)}), s8[4194304]{0:T(1024)(128)(4,1)S(1)}, s32[]{:S(2)}) async-start(s8[7077888]{0:T(1024)(128)(4,1)} %bitcast.295), calls=%async_computation.17 | async-start | bytes 8388608
  338.1 44.5 %reduce-scatter.15.cloned.1.call-start = ((), (), s32[]{:S(2)}) async-start(), calls=%async_computation.12 | async-start | bytes 442368 | tf_op jit(solution)/shard_map/reduce_scatter | solution.py:33
  338.2 5.6 slice-start.2
  384.5 34.1 %all-to-all-start.1 = ((bf16[4,1152,256]{1,2,0:T(8,128)(2,1)}), bf16[4,1152,256]{1,2,0:T(8,128)(2,1)}, u32[]{:S(2)}, u32[]{:S(2)}) async-start(bf16[4,1152,256]{1,2,0:T(8,128)(2,1)} %bitcast.304), calls=%async_computation.5 | async-start | bytes 4718592 | tf_op jit(solution)/shard_map/all_to_all | solution.py:49
  389.0 161.9 %all-gather.7.cloned.1.call-start = ((), (), s32[]{:S(2)}) async-start(), calls=%async_computation.14 | async-start | bytes 4866048 | tf_op jit(solution)/shard_map/all_gather | solution.py:261
  390.9 31.5 %copy-start.51 = (f32[4608]{0:T(1024)S(1)}, f32[4608]{0:T(1024)}, u32[]{:S(2)}) copy-start(f32[4608]{0:T(1024)} %copy-done.47) | copy-start | bytes 55300
  390.9 31.5 %copy-start.63 = (bf16[384,64]{0,1:T(8,128)(2,1)S(1)}, bf16[384,64]{0,1:T(8,128)(2,1)}, u32[]{:S(2)}) copy-start(bf16[384,64]{0,1:T(8,128)(2,1)} %copy-done.62) | copy-start | bytes 147460
  418.6 23.8 %all-to-all-start.2 = ((bf16[4,128,1152]{2,1,0:T(8,128)(2,1)}), bf16[4,128,1152]{2,1,0:T(8,128)(2,1)S(1)}, u32[]{:S(2)}, u32[]{:S(2)}) async-start(bf16[4,128,1152]{2,1,0:T(8,128)(2,1)} %bitcast.294), calls=%async_computation.6 | async-start | bytes 2359296 | tf_op jit(solution)/shard_map/all_to_all | solution.py:49
  442.4 48.9 %all-to-all-start = ((bf16[4,1152,256]{1,2,0:T(8,128)(2,1)}), bf16[4,1152,256]{1,2,0:T(8,128)(2,1)S(1)}, u32[]{:S(2)}, u32[]{:S(2)}) async-start(bf16[4,1152,256]{1,2,0:T(8,128)(2,1)} %bitcast.290), calls=%async_computation.4 | async-start | bytes 4718592 | tf_op jit(solution)/shard_map/all_to_all | solution.py:49
  446.0 5.4 copy-start.56
  (54 other events, 148.2 us)
Sparse Core Ops, SparseCore 0:
  60.2 43.4 reduce-scatter.16
  106.1 44.8 all-reduce.2
  153.9 16.9 reduce-scatter.8
  174.7 82.3 all-gather.4
  288.2 49.8 reduce-scatter.10
  340.4 24.1 reduce-scatter.12
  366.9 15.7 reduce-scatter.14
  392.8 103.7 all-gather.6
where the time goes:
time: 575 us; the launch traced here: 564 us
  waiting for transfers between devices  304 us (53%)
  matrix products  78.5 us (14%)
  local copies, waits for them, and re-layouts  54.9 us (10%)
  blocking collectives  54.7 us (10%)
  starting transfers between devices  27.8 us (5%)
  other arithmetic  27.1 us (5%)
  between operations  16.7 us (3%)
    unnamed x10, waiting for transfers between devices  89.6 us
    all_to_all x4, waiting for transfers between devices, sum_at_owner(): lax.all_to_all(pieces, axis, split_axis=0, concat_axis=0, tiled=True)  76.6 us
    all_gather x2, waiting for transfers between devices, local(): full_upstream = lax.all_gather(local_layer, TP, axis=0, tiled=True)  73.8 us
    reduce_scatter x4, waiting for transfers between devices, sum_in_order(): pieces = lax.psum_scatter(pieces, axes[k], scatter_dimension=0, tiled=True)  61.8 us
    psum x5, blocking collectives, by_axis(): return functools.reduce(lax.psum, axes, x)  54.7 us
    dot_general x12, matrix products, contract_rows(): lax.dot_general(left_side, right_side, (((0,), (0,)), ((), ())), preferre...  38.7 us
    unnamed x171, local copies, waits for them, and re-layouts  24.5 us
    dot_general x12, matrix products, contract_cols(): lax.dot_general(left_side, right_side, (((1,), (1,)), ((), ())), preferre...  16.5 us
  transfers between devices with their start and end apart: 20, of which 11 were waited for; matrix products, arithmetic and copies ran while one was open for 18% of the time, Pallas kernels for 0%

commit v1 on v0

v1 whole, which is shorter than its diff:
```python
import functools
import math

import jax
import jax.numpy as jnp
import numpy as np
from jax import lax
from jax.experimental import pallas as pl
from jax.experimental.pallas import tpu as pltpu
from jax.sharding import Mesh
from jax.sharding import PartitionSpec as P

D = 4608
HEADS = 32
HD = 128
SEQ = 384
LAYERS = 2
CB = D // 4
RB = 48
CA = 640
XL, CORE, Y, XH, Z = ("dp_0", "dp_1", "tp_0", "tp_1", "tp_2")
TP = (Y, XH, Z)
DP = (XL, CORE)
MESH = pl.DeviceIdType.MESH
VMEM = pltpu.VMEM
F32 = jnp.float32
BF16 = jnp.bfloat16

softcap = 50.0
epsilon = 1e-06
score_scale = (D // HEADS) ** (-0.5)


def rope_tables():
    half = HD // 2
    freq = np.exp(-np.arange(half, dtype=np.float64) * (2.0 * math.log(10000.0) / HD))
    angles = np.arange(SEQ, dtype=np.float64)[:, None] * freq[None, :]
    cosine, sine = np.cos(angles), np.sin(angles)
    return (
        np.concatenate([cosine, cosine], axis=1).astype(np.float32),
        np.concatenate([-sine, sine], axis=1).astype(np.float32),
    )


def rotate(v, cosine, sine):
    return v * cosine + pltpu.roll(v, HD // 2, 1) * sine


def unrotate(v, cosine, sine):
    return v * cosine - pltpu.roll(v, HD // 2, 1) * sine


def dot_nn(a, b):
    return lax.dot_general(a, b, (((1,), (0,)), ((), ())), preferred_element_type=F32)


def dot_nt(a, b):
    return lax.dot_general(a, b, (((1,), (1,)), ((), ())), preferred_element_type=F32)


def dot_tn(a, b):
    return lax.dot_general(a, b, (((0,), (0,)), ((), ())), preferred_element_type=F32)


def whole(shape):
    return pl.BlockSpec(shape, lambda *_: (0,) * len(shape), pipeline_mode=pl.Buffered(1))


def at_layer(l, shape):
    return pl.BlockSpec(
        (None, *shape), lambda *_: (l, *(0,) * len(shape)), pipeline_mode=pl.Buffered(1)
    )


def forward_kernel(x, gain, wq, wk, wv, cosine, sine, normed, recip, q, kv, wcat):
    rows = x.shape[0]

    @pl.when(pl.program_id(1) == 0)
    def _():
        @pl.loop(0, D // 512)
        def _(c):
            at = pl.ds(pl.multiple_of(c * 512, 512), 512)
            wcat[at, :HD] = wq[at, :]
            wcat[at, HD:] = jnp.concatenate([wk[at, :], wv[at, :]], axis=1)

    @pl.loop(0, rows // 16)
    def _(r):
        at = pl.ds(pl.multiple_of(r * 16, 16), 16)
        v = x[at, :].astype(F32)
        rc = lax.rsqrt(jnp.sum(v * v, axis=1, keepdims=True) * (1.0 / D) + epsilon)
        normed[at, :] = (v * rc * gain[...]).astype(BF16)
        recip[at, :] = jnp.broadcast_to(rc, (16, HD))

    acc = jnp.zeros((rows, 2 * HD), F32)
    for c in range(3):
        at = slice(c * 1536, (c + 1) * 1536)
        acc = acc + dot_nn(normed[:, at], wcat[at, :])
    q[...] = rotate(acc[:, :HD], cosine[...], sine[...]).astype(BF16)
    kv[...] = acc[:, HD:]


def forward(x, gain, wq, wk, wv, cosine, sine):
    br = 192
    row = lambda l, r: (l, r, 0)
    per_layer = lambda l, r: (l, 0, 0)
    return pl.pallas_call(
        forward_kernel,
        grid=(LAYERS, SEQ // br),
        in_specs=[
            pl.BlockSpec((None, br, D), row),
            pl.BlockSpec((None, 1, D), per_layer),
            pl.BlockSpec((None, D, HD), per_layer),
            pl.BlockSpec((None, D, HD // 2), per_layer),
            pl.BlockSpec((None, D, HD // 2), per_layer),
            pl.BlockSpec((br, HD), lambda l, r: (r, 0)),
            pl.BlockSpec((br, HD), lambda l, r: (r, 0)),
        ],
        out_specs=[
            pl.BlockSpec((None, br, D), row),
            pl.BlockSpec((None, br, HD), row),
            pl.BlockSpec((None, br, HD), row),
            pl.BlockSpec((None, br, HD), row),
            pl.BlockSpec((None, D, 2 * HD), per_layer),
        ],
        out_shape=[
            jax.ShapeDtypeStruct((LAYERS, SEQ, D), BF16),
            jax.ShapeDtypeStruct((LAYERS, SEQ, HD), F32),
            jax.ShapeDtypeStruct((LAYERS, SEQ, HD), BF16),
            jax.ShapeDtypeStruct((LAYERS, SEQ, HD), F32),
            jax.ShapeDtypeStruct((LAYERS, D, 2 * HD), BF16),
        ],
        compiler_params=pltpu.CompilerParams(vmem_limit_bytes=48 * 1024 * 1024),
        name="projections",
    )(x, gain.reshape(LAYERS, 1, D), wq, wk, wv, cosine, sine)


def attention_kernel(
    l, lengths, reach, g, wo, q, own, other, cosine, sine, dq_out, keep_out, send_out, att_out
):
    even = lax.axis_index(Z) % 2 == 0
    lane = lax.broadcasted_iota(jnp.int32, (SEQ, HD), 1)
    low = lane < HD // 2
    cs, sn = cosine[...], sine[...]
    first = jnp.where(even, own[...], other[...])
    second = jnp.where(even, other[...], own[...])
    k_raw = jnp.where(low, first, pltpu.roll(second, HD // 2, 1))
    v_raw = jnp.where(low, pltpu.roll(first, HD // 2, 1), second)
    k = rotate(k_raw, cs, sn).astype(BF16)
    v = v_raw.astype(BF16)

    e0 = lengths[0, 0]
    e1 = e0 + lengths[0, 1]
    e2 = e1 + lengths[0, 2]
    span = reach[l]

    def doc(pos):
        return (
            (pos >= e0).astype(jnp.int32)
            + (pos >= e1).astype(jnp.int32)
            + (pos >= e2).astype(jnp.int32)
        )

    i = lax.broadcasted_iota(jnp.int32, (SEQ, SEQ), 0)
    j = lax.broadcasted_iota(jnp.int32, (SEQ, SEQ), 1)
    doc_i = doc(lax.broadcasted_iota(jnp.int32, (SEQ, 1), 0))
    doc_j = doc(lax.broadcasted_iota(jnp.int32, (1, SEQ), 1))
    allowed = (doc_i == doc_j) & (j <= i) & (i - j < span)

    qq = q[...]
    squashed = jnp.tanh(dot_nt(qq, k) * (score_scale / softcap))
    raised = jnp.where(allowed, jnp.exp(softcap * squashed), 0.0)
    prob = raised / jnp.sum(raised, axis=1, keepdims=True)
    rounded = prob.astype(BF16)
    att = dot_nn(rounded, v).astype(BF16)
    ga = jnp.zeros((SEQ, HD), F32)
    for c in range(3):
        at = slice(c * 1536, (c + 1) * 1536)
        ga = ga + dot_nt(g[:, at], wo[:, at])
    ga = ga.astype(BF16)
    delta = jnp.sum(ga.astype(F32) * att.astype(F32), axis=1, keepdims=True)
    ds = prob * (dot_nt(ga, v) - delta) * (1.0 - squashed * squashed) * score_scale
    ds = ds.astype(BF16)
    dq = unrotate(dot_nn(ds, k), cs, sn)
    dk = unrotate(dot_tn(ds, qq), cs, sn)
    dv = dot_tn(rounded, ga)
    dk_turned, dv_turned = pltpu.roll(dk, HD // 2, 1), pltpu.roll(dv, HD // 2, 1)
    lower = jnp.where(low, dk, dv_turned)
    upper = jnp.where(low, dk_turned, dv)
    dq_out[...] = dq.astype(BF16)
    keep_out[...] = jnp.where(even, lower, upper).astype(BF16)
    send_out[...] = jnp.where(even, upper, lower).astype(BF16)
    att_out[...] = att


def attention(l, lengths, reach, g, wo, q, own, other, cosine, sine):
    smem = pl.BlockSpec(memory_space=pltpu.SMEM)
    small = jax.ShapeDtypeStruct((SEQ, HD), BF16)
    return pl.pallas_call(
        functools.partial(attention_kernel, l),
        grid=(1,),
        in_specs=[
            smem,
            smem,
            whole((SEQ, D)),
            at_layer(l, (HD, D)),
            at_layer(l, (SEQ, HD)),
            at_layer(l, (SEQ, HD)),
            at_layer(l, (SEQ, HD)),
            whole((SEQ, HD)),
            whole((SEQ, HD)),
        ],
        out_specs=[whole((SEQ, HD))] * 4,
        out_shape=[small] * 4,
        compiler_params=pltpu.CompilerParams(vmem_limit_bytes=48 * 1024 * 1024),
        name=f"attention{l}",
    )(lengths, reach, g, wo, q, own, other, cosine, sine)


def add(*parts):
    return functools.reduce(lambda a, b: a + b, [p[...].astype(F32) for p in parts])


class Ring:
    def __init__(self, axis, src, bufs, ss, rs):
        i = lax.axis_index(axis)
        up, dn, far = lax.rem(i + 1, 4), lax.rem(i + 3, 4), lax.rem(i + 2, 4)
        r1p, r1m, r2p, r2m, r3p, r3m, tp, tm = bufs
        plan = [
            (src(far, 0), r1p, up),
            (src(far, 1), r1m, dn),
            (src(up, 1), r2p, up),
            (src(dn, 0), r2m, dn),
            (tp, r3p, up),
            (tm, r3m, dn),
        ]
        self.copies = [
            pltpu.make_async_remote_copy(
                src_ref=s,
                dst_ref=d,
                send_sem=ss.at[n],
                recv_sem=rs.at[n],
                device_id={axis: to},
                device_id_type=MESH,
            )
            for n, (s, d, to) in enumerate(plan)
        ]
        self.i, self.up, self.dn, self.src, self.bufs = i, up, dn, src, bufs

    def start(self):
        for n in range(4):
            self.copies[n].start()

    def middle(self):
        r1p, r1m, _, _, _, _, tp, tm = self.bufs
        self.copies[0].wait_recv()
        tp[...] = add(r1p, self.src(self.up, 0)).astype(BF16)
        self.copies[4].start()
        self.copies[1].wait_recv()
        tm[...] = add(r1m, self.src(self.dn, 1)).astype(BF16)
        self.copies[5].start()

    def finish(self, out):
        _, _, r2p, r2m, r3p, r3m, _, _ = self.bufs
        self.copies[3].wait_recv()
        self.copies[4].wait_recv()
        out(0)[...] = add(self.src(self.i, 0), r3p, r2m).astype(BF16)
        self.copies[2].wait_recv()
        self.copies[5].wait_recv()
        out(1)[...] = add(self.src(self.i, 1), r2p, r3m).astype(BF16)

    def drain(self):
        for c in self.copies:
            c.wait_send()


def exchange_kernel(
    last,
    dq,
    keep,
    send,
    att,
    wcat_hbm,
    normed_hbm,
    g_hbm,
    x_hbm,
    recip,
    gain,
    gain_before,
    g_out,
    dw_out,
    gain_out,
    wcat,
    normed,
    g,
    S,
    T,
    dqkv_t,
    att_t,
    dqkv,
    pair_in,
    x_own,
    a1,
    b1,
    a2,
    b2,
    ua,
    ub,
    va,
    x_in,
    stat_out,
    stat_in,
    core_in,
    xl_out,
    xl_in,
    pack,
    gain_in,
    gain_z,
    gain_y,
    s_pair,
    s_local,
    s_a1,
    s_b1,
    s_a2,
    s_b2,
    s_x,
    s_stat,
    s_core,
    s_xl,
    s_g1,
    s_g2,
    s_g3,
    s_ag_x,
    s_ag,
):
    xl, core, y, xh, z = (lax.axis_index(a) for a in (XL, CORE, Y, XH, Z))

    def remote(src, dst, sems, n, **to):
        return pltpu.make_async_remote_copy(
            src_ref=src,
            dst_ref=dst,
            send_sem=sems.at[0, n],
            recv_sem=sems.at[1, n],
            device_id=to,
            device_id_type=MESH,
        )

    ymates = [{Y: lax.rem(y + k, 4)} for k in (1, 2, 3)]
    zmates = [{Z: lax.rem(z + k, 4)} for k in (1, 2, 3)]
    xmates = [
        {XL: lax.rem(xl + a, 2), CORE: lax.rem(core + b, 2), XH: lax.rem(xh + c, 2)}
        for a in (0, 1)
        for b in (0, 1)
        for c in (0, 1)
        if a + b + c
    ]

    l = 0 if last else 1
    fetch = [
        pltpu.make_async_copy(src, dst, s_local.at[n])
        for n, (src, dst) in enumerate(
            [
                (wcat_hbm.at[l], wcat),
                (normed_hbm.at[l], normed),
                (g_hbm, g),
                (x_hbm.at[l, pl.ds(z * 96 + xh * RB, RB), pl.ds(y * CB, CB)], x_own),
            ]
        )
    ]
    for c in fetch:
        c.start()

    barrier = pltpu.get_barrier_semaphore()
    for to in (*ymates, *zmates, *xmates):
        pl.semaphore_signal(barrier, inc=1, device_id=to, device_id_type=MESH)
    pl.semaphore_wait(barrier, 13)

    pair = remote(send, pair_in, s_pair, 0, **{Z: z + 1 - 2 * lax.rem(z, 2)})
    pair.start()
    dqkv[:, :HD] = dq[...]
    pair.wait_recv()
    dqkv[:, HD:] = add(keep, pair_in).astype(BF16)

    fetch[0].wait()

    @pl.loop(0, D // 512)
    def _(c):
        at = pl.ds(pl.multiple_of(c * 512, 512), 512)
        S[:, :, :, at] = dot_nt(dqkv[...], wcat[at, :]).astype(BF16).reshape(4, 2, RB, 512)

    def cols(t, width=CB, shift=0):
        return pl.ds(pl.multiple_of(t * CB + shift, 128), width)

    ring_a1 = Ring(
        Y,
        lambda t, h: S.at[pl.ds(2 * h, 2), 0, :, cols(t)],
        [a1.at[n] for n in range(8)],
        s_a1.at[0],
        s_a1.at[1],
    )
    ring_b1 = Ring(
        Z,
        lambda t, h: S.at[t, 1, :, pl.ds(h * 2 * CB, 2 * CB)],
        [b1.at[n] for n in range(8)],
        s_b1.at[0],
        s_b1.at[1],
    )
    part = [pl.ds(0, CA), pl.ds(CA, CB - CA)]
    kinds = (0, 1, 1, 0, 0, 1, 0, 1)
    ring_a2 = Ring(
        Z,
        lambda t, h: ua.at[t, :, part[h]],
        [a2.at[n, :, part[h]] for n, h in enumerate(kinds)],
        s_a2.at[0],
        s_a2.at[1],
    )
    ring_b2 = Ring(
        Y,
        lambda t, h: ub.at[:, cols(t, (CA, CB - CA)[h], h * CA)],
        [b2.at[n, :, part[h]] for n, h in enumerate(kinds)],
        s_b2.at[0],
        s_b2.at[1],
    )
    ring_a1.start()
    ring_b1.start()

    dqkv_t[...] = dqkv[...].T
    att_t[...] = att[...].T
    fetch[1].wait()
    fetch[2].wait()

    @pl.loop(0, D // 512)
    def _(c):
        at = pl.ds(pl.multiple_of(c * 512, 512), 512)
        T[: 2 * HD, at] = dot_nn(dqkv_t[...], normed[:, at]).astype(BF16)
        T[2 * HD :, at] = dot_nn(att_t[...], g[:, at]).astype(BF16)

    to_core = [
        remote(
            T.at[:, pl.ds(pl.multiple_of((2 * k + 1 - core) * CB, 128), CB)],
            core_in.at[k],
            s_core,
            k,
            **{CORE: 1 - core},
        )
        for k in (0, 1)
    ]
    to_core[0].start()
    to_core[1].start()

    ring_a1.middle()
    ring_b1.middle()
    ring_a1.finish(lambda h: ua.at[pl.ds(2 * h, 2)])
    ring_a2.start()
    ring_b1.finish(lambda h: ub.at[:, pl.ds(h * 2 * CB, 2 * CB)])
    ring_b2.start()
    ring_a2.middle()
    ring_b2.middle()
    ring_a2.finish(lambda h: va.at[0, :, part[h]])
    ring_b2.finish(lambda h: va.at[1, :, part[h]])
    to_x = remote(va.at[1 - xh], x_in, s_x, 0, **{XH: 1 - xh})
    to_x.start()

    for c in to_core:
        c.wait_recv()

    def dp_cols(k):
        return pl.ds(pl.multiple_of((2 * k + core) * CB, 128), CB)

    @pl.loop(0, SEQ // 32)
    def _(r):
        at = pl.ds(pl.multiple_of(r * 32, 32), 32)
        there = T[at, dp_cols(1 - xl)].astype(F32) + core_in[1 - xl, at, :].astype(F32)
        xl_out[at, :] = there.astype(BF16)

    fetch[3].wait()
    to_x.wait_recv()
    grad = add(va.at[xh], x_in)
    rows = pl.ds(pl.multiple_of(z * 96 + xh * RB, 16), RB)
    rc = recip[rows, :][:, :1]
    gn = gain[:, cols(y)]
    unit = x_own[...].astype(F32) * rc
    u = grad * gn
    stat = jnp.sum(u * unit, axis=1, keepdims=True)
    stat_out[...] = jnp.broadcast_to(stat, (RB, HD))
    to_stat = [remote(stat_out, stat_in.at[n], s_stat, n, **to) for n, to in enumerate(ymates)]
    for c in to_stat:
        c.start()
    per_feature = jnp.sum(grad * unit, axis=0, keepdims=True)
    pack[...] = gain_before[...]
    for n in range(9):
        k = n + 9 if last else n
        pack[k : k + 1, :] = per_feature[:, n * 128 : (n + 1) * 128]
    if last:
        to_g1 = [remote(pack, gain_in.at[n], s_g1, n, **to) for n, to in enumerate(xmates)]
        for c in to_g1:
            c.start()
    else:
        gain_out[...] = pack[...]
    for c in to_stat:
        c.wait_recv()
    mean = (stat_out[...] + stat_in[0] + stat_in[1] + stat_in[2])[:, :1] * (1.0 / D)
    up_own = g[rows, cols(y)].astype(F32)
    g_out[z, xh, :, cols(y)] = (up_own + rc * (u - unit * mean)).astype(BF16)

    def spread(zz, hh, yy, shift, width, n, **to):
        ref = g_out.at[zz, hh, :, cols(yy, width, shift)]
        return remote(ref, ref, s_ag, n, **to)

    def walk(first_axis, hh, base):
        second = Y if first_axis == Z else Z
        i, j = (z, y) if first_axis == Z else (y, z)
        order = [i, lax.rem(i + 3, 4), lax.rem(i + 1, 4), lax.rem(i + 2, 4)]
        up1, dn1 = {first_axis: lax.rem(i + 1, 4)}, {first_axis: lax.rem(i + 3, 4)}
        up2, dn2 = {second: lax.rem(j + 1, 4)}, {second: lax.rem(j + 3, 4)}
        jdn, jup, jfar = lax.rem(j + 3, 4), lax.rem(j + 1, 4), lax.rem(j + 2, 4)

        def one(ii, jj, n, to, shift=0, width=CB):
            zz, yy = (ii, jj) if first_axis == Z else (jj, ii)
            return spread(zz, hh, yy, shift, width, base + n, **to)

        sent = []

        def go(c):
            c.start()
            sent.append(c)

        def begin():
            go(one(order[0], j, 0, up1))
            go(one(order[0], j, 1, dn1))
            go(one(order[0], j, 4, up2))
            go(one(order[0], j, 5, dn2))

        def arrive_dn():
            one(order[1], j, 0, up1).wait_recv()
            go(one(order[1], j, 2, up1, 0, CA))
            go(one(order[1], j, 6, up2))
            go(one(order[1], j, 7, dn2))

        def arrive_up():
            one(order[2], j, 1, dn1).wait_recv()
            go(one(order[2], j, 3, dn1, CA, CB - CA))
            go(one(order[2], j, 8, up2))
            go(one(order[2], j, 9, dn2))

        def arrive_far():
            one(order[3], j, 2, up1, 0, CA).wait_recv()
            one(order[3], j, 3, dn1, CA, CB - CA).wait_recv()
            go(one(order[3], j, 10, up2))
            go(one(order[3], j, 11, dn2))

        def second_step(k):
            one(order[k], jdn, 4 + 2 * k, up2).wait_recv()
            if k in (0, 2):
                go(one(order[k], jdn, 12 + k, up2))
            one(order[k], jup, 5 + 2 * k, dn2).wait_recv()
            if k in (1, 3):
                go(one(order[k], jup, 12 + k, dn2))

        def last_step(k):
            one(order[k], jfar, 12 + k, up2 if k in (0, 2) else dn2).wait_recv()

        def done():
            for c in sent:
                c.wait_send()

        return begin, arrive_dn, arrive_up, arrive_far, second_step, last_step, done

    mine = g_out.at[z, xh, :, cols(y)]
    across = remote(mine, mine, s_ag_x, 0, **{XH: 1 - xh})
    across.start()
    own = walk(Z, xh, 0)
    oth = walk(Y, 1 - xh, 16)
    own[0]()
    to_xl = remote(xl_out, xl_in, s_xl, 0, **{XL: 1 - xl})
    to_xl.start()
    own[1]()
    own[2]()
    theirs = g_out.at[z, 1 - xh, :, cols(y)]
    remote(theirs, theirs, s_ag_x, 0, **{XH: 1 - xh}).wait_recv()
    oth[0]()
    own[4](0)
    own[3]()
    oth[1]()
    oth[2]()
    own[4](1)
    oth[4](0)
    own[4](2)
    oth[3]()
    oth[4](1)
    if last:
        for c in to_g1:
            c.wait_recv()
        total = pack[...]
        for n in range(7):
            total = total + gain_in[n]
        gain_in[7] = total
        to_g2 = [remote(gain_in.at[7], gain_z.at[n], s_g2, n, **t) for n, t in enumerate(zmates)]
        for c in to_g2:
            c.start()
    own[4](3)
    oth[4](2)
    if last:
        for c in to_g2:
            c.wait_recv()
        total = (gain_in[7] + gain_z[0] + gain_z[1] + gain_z[2]) * (1.0 / 4)
        gain_z[3] = total
        to_g3 = [remote(gain_z.at[3], gain_y.at[n], s_g3, n, **t) for n, t in enumerate(ymates)]
        for c in to_g3:
            c.start()
    oth[4](3)
    for k in range(4):
        own[5](k)
        oth[5](k)
    if last:
        for c in to_g3:
            c.wait_recv()
        for n in range(-1, 3):
            ref = gain_z.at[3] if n < 0 else gain_y.at[n]
            yy = lax.rem(y + 3 - n, 4)
            for k in range(9):
                at = pl.ds(pl.multiple_of(yy * CB + k * 128, 128), 128)
                gain_out[1:2, at] = ref[k : k + 1, :]
                gain_out[0:1, at] = ref[9 + k : 10 + k, :]

    to_xl.wait_recv()

    @pl.loop(0, SEQ // 32)
    def _(r):
        at = pl.ds(pl.multiple_of(r * 32, 32), 32)
        here = T[at, dp_cols(xl)].astype(F32) + core_in[xl, at, :].astype(F32)
        dw_out[at, :] = (here + xl_in[at, :].astype(F32)) * (1.0 / 4)

    pair.wait_send()
    for ring in (ring_a1, ring_b1, ring_a2, ring_b2):
        ring.drain()
    to_x.wait_send()
    across.wait_send()
    to_xl.wait_send()
    for c in (*to_core, *to_stat):
        c.wait_send()
    if last:
        for c in (*to_g1, *to_g2, *to_g3):
            c.wait_send()
    own[6]()
    oth[6]()


def exchange(l, dq, keep, send, att, wcat, normed, g, x, recip, gain, gain_before):
    last = l == 0
    sem = pltpu.SemaphoreType.DMA
    gain_shape = (8, D) if last else (24, 128)
    hbm = pl.BlockSpec(memory_space=pl.ANY)
    return pl.pallas_call(
        functools.partial(exchange_kernel, last),
        grid=(1,),
        in_specs=[
            whole((SEQ, HD)),
            whole((SEQ, HD)),
            whole((SEQ, HD)),
            whole((SEQ, HD)),
            hbm,
            hbm,
            hbm,
            hbm,
            at_layer(l, (SEQ, HD)),
            at_layer(l, (1, D)),
            whole((24, 128)),
        ],
        out_specs=[whole((4, 2, RB, D)), whole((SEQ, CB)), whole(gain_shape)],
        out_shape=[
            jax.ShapeDtypeStruct((4, 2, RB, D), BF16),
            jax.ShapeDtypeStruct((SEQ, CB), F32),
            jax.ShapeDtypeStruct(gain_shape, F32),
        ],
        scratch_shapes=[
            VMEM((D, 2 * HD), BF16),
            VMEM((SEQ, D), BF16),
            VMEM((SEQ, D), BF16),
            VMEM((4, 2, RB, D), BF16),
            VMEM((SEQ, D), BF16),
            VMEM((2 * HD, SEQ), BF16),
            VMEM((HD, SEQ), BF16),
            VMEM((SEQ, 2 * HD), BF16),
            VMEM((SEQ, HD), BF16),
            VMEM((RB, CB), BF16),
            VMEM((8, 2, RB, CB), BF16),
            VMEM((8, RB, 2 * CB), BF16),
            VMEM((8, RB, CB), BF16),
            VMEM((8, RB, CB), BF16),
            VMEM((4, RB, CB), BF16),
            VMEM((RB, D), BF16),
            VMEM((2, RB, CB), BF16),
            VMEM((RB, CB), BF16),
            VMEM((RB, HD), F32),
            VMEM((3, RB, HD), F32),
            VMEM((2, SEQ, CB), BF16),
            VMEM((SEQ, CB), BF16),
            VMEM((SEQ, CB), BF16),
            VMEM((24, 128), F32),
            VMEM((8, 24, 128), F32),
            VMEM((4, 24, 128), F32),
            VMEM((3, 24, 128), F32),
            sem((2, 1)),
            sem((4,)),
            sem((2, 6)),
            sem((2, 6)),
            sem((2, 6)),
            sem((2, 6)),
            sem((2, 1)),
            sem((2, 3)),
            sem((2, 2)),
            sem((2, 1)),
            sem((2, 7)),
            sem((2, 3)),
            sem((2, 3)),
            sem((2, 1)),
            sem((2, 32)),
        ],
        compiler_params=pltpu.CompilerParams(
            collective_id=l, has_side_effects=True, vmem_limit_bytes=62 * 1024 * 1024
        ),
        name=f"exchange{l}",
    )(
        dq,
        keep,
        send,
        att,
        wcat,
        normed,
        g,
        x,
        recip,
        gain.reshape(LAYERS, 1, D),
        gain_before,
    )


def local(layer_inputs, out_grad, gain, w_query, w_key, w_value, w_out, doc_lengths, window_reach):
    cosine, sine = (jnp.asarray(t) for t in rope_tables())
    normed, recip, q, kv, wcat = forward(
        layer_inputs, gain, w_query, w_key, w_value, cosine, sine
    )
    kv_other = lax.ppermute(kv, Z, [(i, i ^ 1) for i in range(4)])
    g = out_grad
    gains = jnp.zeros((24, 128), F32)
    grads = [None] * LAYERS
    for l in reversed(range(LAYERS)):
        dq, keep, send, att = attention(
            l, doc_lengths, window_reach, g, w_out, q, kv, kv_other, cosine, sine
        )
        g, grads[l], gains = exchange(
            l, dq, keep, send, att, wcat, normed, g, layer_inputs, recip, gain, gains
        )
        g = g.reshape(SEQ, D)
    grads = jnp.stack(grads)
    qkv = jnp.swapaxes(grads[:, : 2 * HD], 1, 2)
    return (
        g,
        qkv[:, :, :HD],
        qkv[:, :, HD : HD + HD // 2],
        qkv[:, :, HD + HD // 2 :],
        grads[:, 2 * HD :],
        gains[:LAYERS],
    )


def solution(mesh):
    split = Mesh(mesh.devices.reshape(2, 2, 4, 2, 4), (XL, CORE, Y, XH, Z))
    in_specs = (
        P(None, DP, None),
        P(DP, None),
        P(),
        P(None, None, TP),
        P(None, None, TP),
        P(None, None, TP),
        P(None, TP, None),
        P(DP, None),
        P(),
    )
    out_specs = (
        P(DP, None),
        P(None, DP, TP),
        P(None, DP, TP),
        P(None, DP, TP),
        P(None, TP, DP),
        P(),
    )
    return jax.shard_map(local, mesh=split, in_specs=in_specs, out_specs=out_specs, check_vma=False)
```

time: 575 us -> 217 us (0.38); the launches traced: 564 us -> 216 us
  waiting for transfers between devices: 304 us -> 9.11 us
  Pallas kernels: 0 us -> 177 us
  matrix products: 78.5 us -> 0 us
  blocking collectives: 54.7 us -> 0 us
  local copies, waits for them, and re-layouts: 54.9 us -> 24.5 us
  starting transfers between devices: 27.8 us -> 2.03 us
  other arithmetic: 27.1 us -> 2.58 us
  between operations: 16.7 us -> 0.78 us
    pallas_call x0 -> x5, Pallas kernels: none -> 177 us  [the longest x2 151 us: exchange(): pl.pallas_call(functools.partial(exchange_kernel, last), grid=(1,), in_sp...]
    unnamed x10 -> x0, waiting for transfers between devices: 89.6 us -> none
    dot_general x42 -> x0, matrix products: 78.5 us -> none  [the longest x12 38.7 us: contract_rows(): lax.dot_general(left_side, right_side, (((0,), (0,)), ((), ())), preferre...]
    all_to_all x4 -> x0, waiting for transfers between devices: 76.6 us -> none  [sum_at_owner(): lax.all_to_all(pieces, axis, split_axis=0, concat_axis=0, tiled=True)]
    all_gather x2 -> x0, waiting for transfers between devices: 73.8 us -> none  [local(): full_upstream = lax.all_gather(local_layer, TP, axis=0, tiled=True)]
    reduce_scatter x4 -> x0, waiting for transfers between devices: 61.8 us -> none  [sum_in_order(): pieces = lax.psum_scatter(pieces, axes[k], scatter_dimension=0, tiled=True)]
    psum x5 -> x0, blocking collectives: 54.7 us -> none  [by_axis(): return functools.reduce(lax.psum, axes, x)]
    all_to_all x4 -> x0, starting transfers between devices: 16.3 us -> none  [sum_at_owner(): lax.all_to_all(pieces, axis, split_axis=0, concat_axis=0, tiled=True)]
  transfers between devices with their start and end apart: 20 -> 1, of which waited for: 11 -> 1; matrix products, arithmetic and copies ran while one was open for 18% -> 0% of each run, Pallas kernels for 0% -> 0%
where the time goes in v1:
time: 217 us; the launch traced here: 216 us
  Pallas kernels  177 us (82%)
  local copies, waits for them, and re-layouts  24.5 us (11%)
  waiting for transfers between devices  9.11 us (4%)
  other arithmetic  2.58 us (1%)
    pallas_call x2, Pallas kernels, exchange(): pl.pallas_call(functools.partial(exchange_kernel, last), grid=(1,), in_sp...  151 us
    unnamed x42, local copies, waits for them, and re-layouts  20.4 us
    pallas_call x1, Pallas kernels, forward(): pl.pallas_call(forward_kernel, grid=(LAYERS, SEQ // br), in_specs=[pl.Blo...  16.4 us
    pallas_call x2, Pallas kernels, attention(): pl.pallas_call(functools.partial(attention_kernel, l), grid=(1,), in_spec...  9.79 us
    ppermute x1, waiting for transfers between devices, local(): kv_other = lax.ppermute(kv, Z, [(i, i ^ 1) for i in range(4)])  9.11 us
  transfers between devices with their start and end apart: 1, of which 1 were waited for; matrix products, arithmetic and copies ran while one was open for 0% of the time, Pallas kernels for 0%

profile of v1, /device:TPU:0, one launch (start us, length us, event | category | flops | bytes accessed | tf_op | source)
XLA Modules:
  0.0 216.4 jit_solution(5078447675629005396)
XLA Ops:
  0.6 0.8 reshape.23.gain
  1.4 0.0 copy-start.6
  1.4 2.8 %copy.17.wk = bf16[2,4608,64]{2,1,0:T(8,128)(2,1)S(1)} copy(bf16[2,4608,64]{1,2,0:T(8,128)(2,1)} %param.15) | data formatting | bytes 2359296 | tf_op args[4]
  4.2 0.0 copy-start.3
  4.2 0.0 copy-start.4
  4.3 3.7 %copy.18.wv = bf16[2,4608,64]{2,1,0:T(8,128)(2,1)} copy(bf16[2,4608,64]{1,2,0:T(8,128)(2,1)} %param.16) | data formatting | bytes 2359296 | tf_op args[5]
  8.0 0.0 copy-done.6
  8.0 0.0 copy-done.3
  8.0 0.0 copy-done.4
  8.0 0.0 copy-start.2
  8.0 1.7 copy-done.2
  9.7 0.0 copy-start
  9.7 0.0 copy-start.15
  9.7 0.0 copy-start.16
  9.7 16.4 %projections.1 = (bf16[2,384,4608]{2,1,0:T(8,128)(2,1)}, f32[2,384,128]{2,1,0:T(8,128)S(1)}, bf16[2,384,128]{2,1,0:T(8,128)(2,1)S(1)}, f32[2,384,128]{2,1,0:T(8,128)S(1)}, bf16[2,4608,256]{2,1,0:T(8,128)(2,1)}) custom-call(bf16[2,384,4608]{2,1,0:T(8,128)(2,1)} %x_hbm.3, f32[2,1,4608]{2,1,0:T(1,128)S(1)} %reshape.23.gain, ...), custom_call_target="tpu_custom_call" | custom-call | tf_op jit(solution)/shard_map/projections/pallas_call | solution.py:106
  26.1 2.0 collective-permute-start
  28.2 9.1 %collective-permute-done.other = f32[2,384,128]{2,1,0:T(8,128)S(1)} collective-permute-done((f32[2,384,128]{2,1,0:T(8,128)S(1)}, f32[2,384,128]{2,1,0:T(8,128)S(1)}, u32[]{:S(2)}, u32[]{:S(2)}) %collective-permute-start) | collective-permute-done | bytes 393248 | tf_op jit(solution)/shard_map/ppermute | solution.py:743
  37.3 0.0 copy-done
  37.3 0.0 copy-done.15
  37.3 0.0 copy-done.16
  37.3 4.9 %attention1.1 = (bf16[384,128]{1,0:T(8,128)(2,1)S(1)}, bf16[384,128]{1,0:T(8,128)(2,1)S(1)}, bf16[384,128]{1,0:T(8,128)(2,1)S(1)}, bf16[384,128]{1,0:T(8,128)(2,1)S(1)}) custom-call(s32[1,4]{1,0:T(1,128)S(1)} %copy-done.15, s32[2]{0:T(128)S(1)} %copy-done.16, bf16[384,4608]{1,0:T(8,128)(2,1)} %g_hbm.1, bf16[2,128,4608]{2,1,0:T(8,128)(2,1)S(1)} %copy-done, ...), custom_call_target="tpu_custom_call" | custom-call | tf_op jit(solution)/shard_map/attention1/pallas_call | solution.py:198
  42.2 0.0 copy-done.5
  42.2 0.0 copy-start.11
  42.2 0.6 copy-done.11
  42.9 0.6 copy-done.12
  43.5 0.6 copy-done.13
  44.1 0.6 copy-done.14
  44.8 0.6 broadcast_in_dim.3.gain_before
  45.4 75.9 %exchange1.1 = (bf16[4,2,48,4608]{3,2,1,0:T(8,128)(2,1)}, f32[384,1152]{1,0:T(8,128)}, f32[24,128]{1,0:T(8,128)}) custom-call(bf16[384,128]{1,0:T(8,128)(2,1)} %copy-done.11, bf16[384,128]{1,0:T(8,128)(2,1)} %copy-done.12, bf16[384,128]{1,0:T(8,128)(2,1)} %copy-done.13, bf16[384,128]{1,0:T(8,128)(2,1)} %copy-done.14, ...), custom_call_target="tpu_custom_call" | custom-call | tf_op jit(solution)/shard_map/exchange1/pallas_call | solution.py:653
  121.3 0.0 copy-start.1
  121.3 1.7 copy-done.1
  123.0 4.9 %attention0.1 = (bf16[384,128]{1,0:T(8,128)(2,1)S(1)}, bf16[384,128]{1,0:T(8,128)(2,1)S(1)}, bf16[384,128]{1,0:T(8,128)(2,1)S(1)}, bf16[384,128]{1,0:T(8,128)(2,1)S(1)}) custom-call(s32[1,4]{1,0:T(1,128)S(1)} %copy-done.15, s32[2]{0:T(128)S(1)} %copy-done.16, bf16[384,4608]{1,0:T(8,128)(2,1)} %bitcast.6, bf16[2,128,4608]{2,1,0:T(8,128)(2,1)S(1)} %copy-done.1, ...), custom_call_target="tpu_custom_call" | custom-call | tf_op jit(solution)/shard_map/attention0/pallas_call | solution.py:198
  127.8 0.0 copy-start.7
  127.9 0.6 copy-done.7
  128.5 0.6 copy-done.8
  129.1 0.6 copy-done.9
  129.8 0.6 copy-done.10
  130.4 75.2 %exchange0.1 = (bf16[4,2,48,4608]{3,2,1,0:T(8,128)(2,1)}, f32[384,1152]{1,0:T(8,128)}, f32[8,4608]{1,0:T(8,128)}) custom-call(bf16[384,128]{1,0:T(8,128)(2,1)} %copy-done.7, bf16[384,128]{1,0:T(8,128)(2,1)} %copy-done.8, bf16[384,128]{1,0:T(8,128)(2,1)} %copy-done.9, bf16[384,128]{1,0:T(8,128)(2,1)} %copy-done.10, ...), custom_call_target="tpu_custom_call" | custom-call | tf_op jit(solution)/shard_map/exchange0/pallas_call | solution.py:653
  205.6 0.0 copy-done.17
  205.6 0.0 copy-start.18
  205.6 2.3 %pad_maximum_fusion = f32[2,128,1152]{2,1,0:T(8,128)} fusion(f32[1,384,1152]{2,1,0:T(8,128)S(1)} %bitcast.8, f32[1,384,1152]{2,1,0:T(8,128)} %bitcast.10), kind=kLoop, calls=%fused_computation.4 | loop fusion | flops 294912 | bytes 4718592 | tf_op jit(solution)/shard_map/stack | solution.py:755
  207.9 0.0 copy-done.18
  207.9 0.3 fusion.1
  208.2 0.1 slice.26
  208.3 1.1 fusion.2
  209.4 1.5 slice.23
  210.9 1.4 copy.19
  212.3 4.0 %copy.21 = bf16[384,4608]{1,0:T(8,128)(2,1)} copy(bf16[384,4608]{1,0:T(8,128)(2,1)} %bitcast.12) | data formatting | bytes 7077888
  (8 shorter events, 0.0 us)
Async XLA Ops:
  1.4 6.6 %copy-start.6 = (f32[2,1,4608]{2,1,0:T(1,128)}, f32[2,1,4608]{2,1,0:T(1,128)S(1)}, u32[]{:S(2)}) copy-start(f32[2,1,4608]{2,1,0:T(1,128)S(1)} %reshape.23.gain) | copy-start | bytes 110596
  4.2 3.8 %copy-start.3 = (f32[384,128]{1,0:T(8,128)S(1)}, f32[384,128]{1,0:T(8,128)}, u32[]{:S(2)}) copy-start(f32[384,128]{1,0:T(8,128)} %constant.7.clone.sine) | copy-start | bytes 589828
  4.2 3.8 %copy-start.4 = (f32[384,128]{1,0:T(8,128)S(1)}, f32[384,128]{1,0:T(8,128)}, u32[]{:S(2)}) copy-start(f32[384,128]{1,0:T(8,128)} %constant.6.clone.cosine) | copy-start | bytes 589828
  8.0 1.7 copy-start.2
  9.7 27.6 %copy-start = (bf16[2,128,4608]{2,1,0:T(8,128)(2,1)S(1)}, bf16[2,128,4608]{2,1,0:T(8,128)(2,1)}, u32[]{:S(2)}) copy-start(bf16[2,128,4608]{2,1,0:T(8,128)(2,1)} %wo.3) | copy-start | bytes 7077892
  9.7 27.6 %copy-start.15 = (s32[1,4]{1,0:T(1,128)S(1)}, s32[1,4]{1,0:T(1,128)}, u32[]{:S(2)}) copy-start(s32[1,4]{1,0:T(1,128)} %lengths.3) | copy-start | bytes 52
  9.7 27.6 %copy-start.16 = (s32[2]{0:T(128)S(1)}, s32[2]{0:T(128)}, u32[]{:S(2)}) copy-start(s32[2]{0:T(128)} %reach.3) | copy-start | bytes 28
  26.1 16.1 %copy-start.5 = (f32[2,384,128]{2,1,0:T(8,128)}, f32[2,384,128]{2,1,0:T(8,128)S(1)}, u32[]{:S(2)}) copy-start(f32[2,384,128]{2,1,0:T(8,128)S(1)} %get-tuple-element.33.recip) | copy-start | bytes 1179652
  26.1 11.1 %collective-permute-start = (f32[2,384,128]{2,1,0:T(8,128)S(1)}, f32[2,384,128]{2,1,0:T(8,128)S(1)}, u32[]{:S(2)}, u32[]{:S(2)}) collective-permute-start(f32[2,384,128]{2,1,0:T(8,128)S(1)} %get-tuple-element.26.own), channel_id=1, source_target_pairs={{0,1},{1,0},{2,3},{3,2},{4,5},{5,4},{6,7},{7,6},{8,9},{9,8},{10,11... | collective-permute-start | bytes 1179656 | tf_op jit(solution)/shard_map/ppermute | solution.py:743
  42.2 0.6 copy-start.11
  42.8 0.6 copy-start.12
  43.5 0.6 copy-start.13
  44.1 0.6 copy-start.14
  121.3 1.7 copy-start.1
  127.8 0.6 copy-start.7
  128.5 0.6 copy-start.8
  129.1 0.6 copy-start.9
  129.8 0.6 copy-start.10
  130.4 75.2 %copy-start.17 = (f32[384,1152]{1,0:T(8,128)S(1)}, f32[384,1152]{1,0:T(8,128)}, u32[]{:S(2)}) copy-start(f32[384,1152]{1,0:T(8,128)} %get-tuple-element.42) | copy-start | bytes 5308420
  205.6 2.3 %copy-start.18 = (f32[384,1152]{1,0:T(8,128)S(1)}, f32[384,1152]{1,0:T(8,128)}, u32[]{:S(2)}) copy-start(f32[384,1152]{1,0:T(8,128)} %get-tuple-element.41) | copy-start | bytes 5308420

commit v2 on v0

v2 whole, which is shorter than its diff:
```python
import functools
import math

import jax
import jax.numpy as jnp
import numpy as np
from jax import lax
from jax.experimental import pallas as pl
from jax.experimental.pallas import tpu as pltpu
from jax.sharding import Mesh
from jax.sharding import PartitionSpec as P

D = 4608
HEADS = 32
HD = 128
SEQ = 384
LAYERS = 2
CB = D // 4
RB = 48
CA = 640
XL, CORE, Y, XH, Z = ("dp_0", "dp_1", "tp_0", "tp_1", "tp_2")
TP = (Y, XH, Z)
DP = (XL, CORE)
MESH = pl.DeviceIdType.MESH
VMEM = pltpu.VMEM
F32 = jnp.float32
BF16 = jnp.bfloat16
VMEM_LIMIT = 54 * 1024 * 1024

softcap = 50.0
epsilon = 1e-06
score_scale = (D // HEADS) ** (-0.5)


def rope_tables():
    half = HD // 2
    freq = np.exp(-np.arange(half, dtype=np.float64) * (2.0 * math.log(10000.0) / HD))
    angles = np.arange(SEQ, dtype=np.float64)[:, None] * freq[None, :]
    cosine, sine = np.cos(angles), np.sin(angles)
    return (
        np.concatenate([cosine, cosine], axis=1).astype(np.float32),
        np.concatenate([-sine, sine], axis=1).astype(np.float32),
    )


def rotate(v, cosine, sine):
    return v * cosine + pltpu.roll(v, HD // 2, 1) * sine


def unrotate(v, cosine, sine):
    return v * cosine - pltpu.roll(v, HD // 2, 1) * sine


def dot_nn(a, b):
    return lax.dot_general(a, b, (((1,), (0,)), ((), ())), preferred_element_type=F32)


def dot_nt(a, b):
    return lax.dot_general(a, b, (((1,), (1,)), ((), ())), preferred_element_type=F32)


def dot_tn(a, b):
    return lax.dot_general(a, b, (((0,), (0,)), ((), ())), preferred_element_type=F32)


def add(*parts):
    return functools.reduce(lambda a, b: a + b, [p[...].astype(F32) for p in parts])


class Ring:
    def __init__(self, axis, src, bufs, ss, rs):
        i = lax.axis_index(axis)
        up, dn, far = lax.rem(i + 1, 4), lax.rem(i + 3, 4), lax.rem(i + 2, 4)
        r1p, r1m, r2p, r2m, r3p, r3m, tp, tm = bufs
        plan = [
            (src(far, 0), r1p, up),
            (src(far, 1), r1m, dn),
            (src(up, 1), r2p, up),
            (src(dn, 0), r2m, dn),
            (tp, r3p, up),
            (tm, r3m, dn),
        ]
        self.copies = [
            pltpu.make_async_remote_copy(
                src_ref=s,
                dst_ref=d,
                send_sem=ss.at[n],
                recv_sem=rs.at[n],
                device_id={axis: to},
                device_id_type=MESH,
            )
            for n, (s, d, to) in enumerate(plan)
        ]
        self.i, self.up, self.dn, self.src, self.bufs = i, up, dn, src, bufs

    def start(self, which):
        for n in which:
            self.copies[n].start()

    def middle(self):
        r1p, r1m, _, _, _, _, tp, tm = self.bufs
        self.copies[0].wait_recv()
        tp[...] = add(r1p, self.src(self.up, 0)).astype(BF16)
        self.copies[4].start()
        self.copies[1].wait_recv()
        tm[...] = add(r1m, self.src(self.dn, 1)).astype(BF16)
        self.copies[5].start()

    def finish(self, out):
        _, _, r2p, r2m, r3p, r3m, _, _ = self.bufs
        self.copies[3].wait_recv()
        self.copies[4].wait_recv()
        out(0)[...] = add(self.src(self.i, 0), r3p, r2m).astype(BF16)
        self.copies[2].wait_recv()
        self.copies[5].wait_recv()
        out(1)[...] = add(self.src(self.i, 1), r2p, r3m).astype(BF16)

    def drain(self):
        for c in self.copies:
            c.wait_send()


def write_kernel(*refs):
    *refs, sems = refs
    n = len(refs) // 2
    copies = [pltpu.make_async_copy(refs[k], refs[n + k], sems.at[k]) for k in range(n)]
    for c in copies:
        c.start()
    for c in copies:
        c.wait()


def write_out(*arrays):
    arrays = [pltpu.with_memory_space_constraint(a, pltpu.VMEM) for a in arrays]
    return pl.pallas_call(
        write_kernel,
        in_specs=[pl.BlockSpec(memory_space=pltpu.VMEM)] * len(arrays),
        out_specs=[pl.BlockSpec(memory_space=pl.ANY)] * len(arrays),
        out_shape=[jax.ShapeDtypeStruct(a.shape, a.dtype) for a in arrays],
        scratch_shapes=[pltpu.SemaphoreType.DMA((len(arrays),))],
        compiler_params=pltpu.CompilerParams(vmem_limit_bytes=1024 * 1024),
        name="write_out",
    )(*arrays)


def step_kernel(
    lengths,
    reach,
    x_hbm,
    g_hbm,
    gain,
    wq_hbm,
    wk_hbm,
    wv_hbm,
    wo_hbm,
    cosine,
    sine,
    g_out,
    dwq,
    dwk,
    dwv,
    dwo,
    gain_out,
    m,
):
    xl, core, y, xh, z = (lax.axis_index(a) for a in (XL, CORE, Y, XH, Z))
    half = HD // 2

    def remote(src, dst, sems, n, **to):
        return pltpu.make_async_remote_copy(
            src_ref=src,
            dst_ref=dst,
            send_sem=sems.at[0, n],
            recv_sem=sems.at[1, n],
            device_id=to,
            device_id_type=MESH,
        )

    def rows_of(zz, hh):
        return pl.ds(pl.multiple_of(zz * 96 + hh * RB, 16), RB)

    def cols(t, width=CB, shift=0):
        return pl.ds(pl.multiple_of(t * CB + shift, 128), width)

    ymates = [{Y: lax.rem(y + k, 4)} for k in (1, 2, 3)]
    zmates = [{Z: lax.rem(z + k, 4)} for k in (1, 2, 3)]
    xmates = [
        {XL: lax.rem(xl + a, 2), CORE: lax.rem(core + b, 2), XH: lax.rem(xh + c, 2)}
        for a in (0, 1)
        for b in (0, 1)
        for c in (0, 1)
        if a + b + c
    ]
    pair = {Z: z + 1 - 2 * lax.rem(z, 2)}
    even = lax.rem(z, 2) == 0

    def fetch(n, src, dst):
        return pltpu.make_async_copy(src, dst, m["s_local"].at[n])

    get_x, get_wkv, get_wq, get_wo, get_own = {}, {}, {}, {}, {}
    for l in (1, 0):
        get_x[l] = [
            fetch(16 * l + c, x_hbm.at[l, pl.ds(c * 96, 96)], m["x"].at[c % 2])
            for c in range(4)
        ]
        get_wkv[l] = [
            fetch(16 * l + 4, wk_hbm.at[l], m["wkv"].at[pl.ds(0, half)]),
            fetch(16 * l + 5, wv_hbm.at[l], m["wkv"].at[pl.ds(half, half)]),
        ]
        get_wq[l] = fetch(16 * l + 6, wq_hbm.at[l], m["wq"])
        get_wo[l] = fetch(16 * l + 7, wo_hbm.at[l], m["wo"])
        get_own[l] = fetch(16 * l + 8, x_hbm.at[l, rows_of(z, xh), cols(y)], m["x_own"].at[l])
    get_g = fetch(9, g_hbm, m["g0"])
    for c in (*get_x[1][:2], *get_wkv[1], get_wq[1], get_wo[1], get_g, get_own[1]):
        c.start()
    get_own[0].start()

    barrier = pltpu.get_barrier_semaphore()
    for to in (*ymates, *zmates, *xmates):
        pl.semaphore_signal(barrier, inc=1, device_id=to, device_id_type=MESH)

    kv_pair = [remote(m["kv_send"].at[l], m["kv_in"].at[l], m["s_kv"].at[l], 0, **pair) for l in (0, 1)]
    cs, sn = cosine, sine

    def front(l):
        x, normed = m["x"], m["normed"]
        for c in range(4):
            get_x[l][c].wait()

            @pl.loop(0, 6)
            def _(r):
                at = pl.ds(pl.multiple_of(c * 96 + r * 16, 16), 16)
                v = x[c % 2, pl.ds(pl.multiple_of(r * 16, 16), 16), :].astype(F32)
                rc = lax.rsqrt(jnp.sum(v * v, axis=1, keepdims=True) * (1.0 / D) + epsilon)
                normed[at, :] = (v * rc * gain[l : l + 1, :]).astype(BF16)
                m["recip"][l, at, :] = jnp.broadcast_to(rc, (16, HD))

            if c < 2:
                get_x[l][c + 2].start()
            elif l == 1:
                get_x[0][c - 2].start()

        for c in get_wkv[l]:
            c.wait()
        acc = jnp.zeros((SEQ, HD), F32)
        for c in range(3):
            at = slice(c * 1536, (c + 1) * 1536)
            acc = acc + dot_nt(normed[:, at], m["wkv"][:, at])
        m["kv"][...] = acc
        m["kv_send"][l] = acc.astype(BF16)
        if l == 1:
            pl.semaphore_wait(barrier, 13)
        kv_pair[l].start()
        get_wq[l].wait()
        acc = jnp.zeros((SEQ, HD), F32)
        for c in range(3):
            at = slice(c * 1536, (c + 1) * 1536)
            acc = acc + dot_nn(normed[:, at], m["wq"][at, :])
        m["q"][...] = rotate(acc, cs[...], sn[...]).astype(BF16)

    low = lax.broadcasted_iota(jnp.int32, (SEQ, HD), 1) < half

    def attention(l, g):
        if l == 1:
            get_g.wait()
        get_wo[l].wait()
        ga = jnp.zeros((SEQ, HD), F32)
        for c in range(3):
            at = slice(c * 1536, (c + 1) * 1536)
            ga = ga + dot_nt(g[:, at], m["wo"][:, at])
        ga = ga.astype(BF16)

        kv_pair[l].wait_recv()
        own, other = m["kv"][...], m["kv_in"][l].astype(F32)
        first = jnp.where(even, own, other)
        second = jnp.where(even, other, own)
        k_raw = jnp.where(low, first, pltpu.roll(second, half, 1))
        v_raw = jnp.where(low, pltpu.roll(first, half, 1), second)
        k = rotate(k_raw, cs[...], sn[...]).astype(BF16)
        v = v_raw.astype(BF16)

        e0 = lengths[0, 0]
        e1 = e0 + lengths[0, 1]
        e2 = e1 + lengths[0, 2]
        span = reach[l]

        def doc(pos):
            return (
                (pos >= e0).astype(jnp.int32)
                + (pos >= e1).astype(jnp.int32)
                + (pos >= e2).astype(jnp.int32)
            )

        i = lax.broadcasted_iota(jnp.int32, (SEQ, SEQ), 0)
        j = lax.broadcasted_iota(jnp.int32, (SEQ, SEQ), 1)
        doc_i = doc(lax.broadcasted_iota(jnp.int32, (SEQ, 1), 0))
        doc_j = doc(lax.broadcasted_iota(jnp.int32, (1, SEQ), 1))
        allowed = (doc_i == doc_j) & (j <= i) & (i - j < span)

        q = m["q"][...]
        squashed = jnp.tanh(dot_nt(q, k) * (score_scale / softcap))
        raised = jnp.where(allowed, jnp.exp(softcap * squashed), 0.0)
        prob = raised / jnp.sum(raised, axis=1, keepdims=True)
        rounded = prob.astype(BF16)
        att = dot_nn(rounded, v).astype(BF16)
        delta = jnp.sum(ga.astype(F32) * att.astype(F32), axis=1, keepdims=True)
        ds = prob * (dot_nt(ga, v) - delta) * (1.0 - squashed * squashed) * score_scale
        ds = ds.astype(BF16)
        dk = unrotate(dot_tn(ds, q), cs[...], sn[...])
        dv = dot_tn(rounded, ga)
        lower = jnp.where(low, dk, pltpu.roll(dv, half, 1))
        upper = jnp.where(low, pltpu.roll(dk, half, 1), dv)
        m["keep"][...] = jnp.where(even, lower, upper).astype(BF16)
        m["send"][l] = jnp.where(even, upper, lower).astype(BF16)
        dkv_pair[l].start()
        dq = unrotate(dot_nn(ds, k), cs[...], sn[...]).astype(BF16)
        m["dq"][...] = dq
        m["dq_t"][...] = dq.T
        m["att_t"][...] = att.T

    dkv_pair = [remote(m["send"].at[l], m["dkv_in"].at[l], m["s_dkv"].at[l], 0, **pair) for l in (0, 1)]

    S, T = m["S"], m["T"]
    part = [pl.ds(0, CA), pl.ds(CA, CB - CA)]
    kinds = (0, 1, 1, 0, 0, 1, 0, 1)

    def dp_cols(k):
        return pl.ds(pl.multiple_of((2 * k + core) * CB, 128), CB)

    def finish_weights(l, to_xl):
        to_xl.wait_recv()

        @pl.loop(0, 9)
        def _(k):
            at = pl.ds(pl.multiple_of(k * 128, 128), 128)
            v = (m["dw"][:, at] + m["xl_in"][l, :, at].astype(F32)) * (1.0 / 4)
            dwq[l, at, :] = v[:HD].T
            dwk[l, :, at] = v[HD : HD + half]
            dwv[l, :, at] = v[HD + half : 2 * HD]
            dwo[l, :, at] = v[2 * HD :]

    front(1)
    pack = m["pack"]
    pack[...] = jnp.zeros((24, 128), F32)
    to_xl = {}
    waiting = []
    for l in (1, 0):
        last = l == 0
        g, to = (m["g1"], g_out) if last else (m["g0"], m["g1"])
        attention(l, g)
        if not last:
            get_wo[0].start()
        normed = m["normed"]

        @pl.loop(0, D // 512)
        def _(c):
            at = pl.ds(pl.multiple_of(c * 512, 512), 512)
            T[:HD, at] = dot_nn(m["dq_t"][...], normed[:, at]).astype(BF16)
            T[2 * HD :, at] = dot_nn(m["att_t"][...], g[:, at]).astype(BF16)

        dkv_pair[l].wait_recv()
        dkv = add(m["keep"], m["dkv_in"].at[l]).astype(BF16)
        m["dkv"][...] = dkv
        m["dkv_t"][...] = dkv.T

        sa1, sb1, sa2, sb2 = (m[n].at[l] for n in ("s_a1", "s_b1", "s_a2", "s_b2"))
        ua, ub, va = m["ua"], m["ub"], m["va"]
        ring_a1 = Ring(
            Y,
            lambda t, h: S.at[pl.ds(2 * h, 2), 0, :, cols(t)],
            [m["a1"].at[n] for n in range(8)],
            sa1.at[0],
            sa1.at[1],
        )
        ring_b1 = Ring(
            Z,
            lambda t, h: S.at[t, 1, :, pl.ds(h * 2 * CB, 2 * CB)],
            [m["b1"].at[n] for n in range(8)],
            sb1.at[0],
            sb1.at[1],
        )
        ring_a2 = Ring(
            Z,
            lambda t, h: ua.at[t, :, part[h]],
            [m["a2"].at[n, :, part[h]] for n, h in enumerate(kinds)],
            sa2.at[0],
            sa2.at[1],
        )
        ring_b2 = Ring(
            Y,
            lambda t, h: ub.at[:, cols(t, (CA, CB - CA)[h], h * CA)],
            [m["b2"].at[n, :, part[h]] for n, h in enumerate(kinds)],
            sb2.at[0],
            sb2.at[1],
        )

        for k, starts in ((2, (0, 1)), (1, (2,)), (3, (3,)), (0, ())):

            @pl.loop(0, 3)
            def _(c):
                at = pl.ds(pl.multiple_of(lax.rem(y + k, 4) * CB + c * 384, 128), 384)
                v = dot_nt(m["dq"][...], m["wq"][at, :])
                v = v + dot_nn(m["dkv"][...], m["wkv"][:, at])
                S[:, :, :, at] = v.astype(BF16).reshape(4, 2, RB, 384)

            ring_a1.start(starts)
        ring_b1.start(range(4))
        if not last:
            for c in (*get_wkv[0], get_wq[0]):
                c.start()

        @pl.loop(0, D // 512)
        def _(c):
            at = pl.ds(pl.multiple_of(c * 512, 512), 512)
            T[HD : 2 * HD, at] = dot_nn(m["dkv_t"][...], normed[:, at]).astype(BF16)

        to_core = [
            remote(
                T.at[:, pl.ds(pl.multiple_of((2 * k + 1 - core) * CB, 128), CB)],
                m["core_in"].at[l, k],
                m["s_core"].at[l],
                k,
                **{CORE: 1 - core},
            )
            for k in (0, 1)
        ]
        to_core[0].start()
        to_core[1].start()

        ring_a1.middle()
        ring_b1.middle()
        if last:
            finish_weights(1, to_xl[1])
        else:
            front(0)
        ring_a1.finish(lambda h: ua.at[pl.ds(2 * h, 2)])
        ring_a2.start(range(4))
        ring_b1.finish(lambda h: ub.at[:, pl.ds(h * 2 * CB, 2 * CB)])
        ring_b2.start(range(4))
        ring_a2.middle()
        ring_b2.middle()
        ring_a2.finish(lambda h: va.at[0, :, part[h]])
        ring_b2.finish(lambda h: va.at[1, :, part[h]])
        to_x = remote(va.at[1 - xh], m["x_in"], m["s_x"].at[l], 0, **{XH: 1 - xh})
        to_x.start()

        for c in to_core:
            c.wait_recv()
        xl_out = m["xl_out"]
        if last:
            to_xl[1].wait_send()

        @pl.loop(0, SEQ // 32)
        def _(r):
            at = pl.ds(pl.multiple_of(r * 32, 32), 32)
            there = T[at, dp_cols(1 - xl)].astype(F32) + m["core_in"][l, 1 - xl, at, :].astype(F32)
            xl_out[at, :] = there.astype(BF16)

        get_own[l].wait()
        to_x.wait_recv()
        rows = rows_of(z, xh)
        grad = add(va.at[xh], m["x_in"])
        rc = m["recip"][l, rows, :][:, :1]
        gn = gain[l : l + 1, cols(y)]
        unit = m["x_own"][l].astype(F32) * rc
        u = grad * gn
        stat = jnp.sum(u * unit, axis=1, keepdims=True)
        m["stat_out"][l] = jnp.broadcast_to(stat, (RB, HD))
        to_stat = [
            remote(m["stat_out"].at[l], m["stat_in"].at[l, n], m["s_stat"].at[l], n, **t)
            for n, t in enumerate(ymates)
        ]
        for c in to_stat:
            c.start()
        per_feature = jnp.sum(grad * unit, axis=0, keepdims=True)
        for n in range(9):
            k = n + 9 if last else n
            pack[k : k + 1, :] = per_feature[:, n * 128 : (n + 1) * 128]
        if last:
            gain_in, gain_z, gain_y = m["gain_in"], m["gain_z"], m["gain_y"]
            to_g1 = [
                remote(pack, gain_in.at[n], m["s_g1"], n, **t) for n, t in enumerate(xmates)
            ]
            for c in to_g1:
                c.start()
        for c in to_stat:
            c.wait_recv()
        total = m["stat_out"][l]
        for n in range(3):
            total = total + m["stat_in"][l, n]
        mean = total[:, :1] * (1.0 / D)
        up_own = g[rows, cols(y)].astype(F32)
        to[rows, cols(y)] = (up_own + rc * (u - unit * mean)).astype(BF16)

        def spread(zz, hh, yy, shift, width, n, dest):
            ref = to.at[rows_of(zz, hh), cols(yy, width, shift)]
            return remote(ref, ref, m["s_ag"].at[l], n, **dest)

        def walk(first_axis, hh, base):
            second = Y if first_axis == Z else Z
            i, j = (z, y) if first_axis == Z else (y, z)
            order = [i, lax.rem(i + 3, 4), lax.rem(i + 1, 4), lax.rem(i + 2, 4)]
            up1, dn1 = {first_axis: lax.rem(i + 1, 4)}, {first_axis: lax.rem(i + 3, 4)}
            up2, dn2 = {second: lax.rem(j + 1, 4)}, {second: lax.rem(j + 3, 4)}
            jdn, jup, jfar = lax.rem(j + 3, 4), lax.rem(j + 1, 4), lax.rem(j + 2, 4)

            def one(ii, jj, n, dest, shift=0, width=CB):
                zz, yy = (ii, jj) if first_axis == Z else (jj, ii)
                return spread(zz, hh, yy, shift, width, base + n, dest)

            sent = []

            def go(c):
                c.start()
                sent.append(c)

            def begin():
                go(one(order[0], j, 0, up1))
                go(one(order[0], j, 1, dn1))
                go(one(order[0], j, 4, up2))
                go(one(order[0], j, 5, dn2))

            def arrive_dn():
                one(order[1], j, 0, up1).wait_recv()
                go(one(order[1], j, 2, up1, 0, CA))
                go(one(order[1], j, 6, up2))
                go(one(order[1], j, 7, dn2))

            def arrive_up():
                one(order[2], j, 1, dn1).wait_recv()
                go(one(order[2], j, 3, dn1, CA, CB - CA))
                go(one(order[2], j, 8, up2))
                go(one(order[2], j, 9, dn2))

            def arrive_far():
                one(order[3], j, 2, up1, 0, CA).wait_recv()
                one(order[3], j, 3, dn1, CA, CB - CA).wait_recv()
                go(one(order[3], j, 10, up2))
                go(one(order[3], j, 11, dn2))

            def second_step(k):
                one(order[k], jdn, 4 + 2 * k, up2).wait_recv()
                if k in (0, 2):
                    go(one(order[k], jdn, 12 + k, up2))
                one(order[k], jup, 5 + 2 * k, dn2).wait_recv()
                if k in (1, 3):
                    go(one(order[k], jup, 12 + k, dn2))

            def last_step(k):
                one(order[k], jfar, 12 + k, up2 if k in (0, 2) else dn2).wait_recv()

            def done():
                for c in sent:
                    c.wait_send()

            return begin, arrive_dn, arrive_up, arrive_far, second_step, last_step, done

        mine = to.at[rows, cols(y)]
        across = remote(mine, mine, m["s_ag_x"].at[l], 0, **{XH: 1 - xh})
        across.start()
        own = walk(Z, xh, 0)
        oth = walk(Y, 1 - xh, 16)
        own[0]()
        to_xl[l] = remote(xl_out, m["xl_in"].at[l], m["s_xl"].at[l], 0, **{XL: 1 - xl})
        to_xl[l].start()

        @pl.loop(0, SEQ // 32)
        def _(r):
            at = pl.ds(pl.multiple_of(r * 32, 32), 32)
            here = T[at, dp_cols(xl)].astype(F32) + m["core_in"][l, xl, at, :].astype(F32)
            m["dw"][at, :] = here

        own[1]()
        own[2]()
        theirs = to.at[rows_of(z, 1 - xh), cols(y)]
        remote(theirs, theirs, m["s_ag_x"].at[l], 0, **{XH: 1 - xh}).wait_recv()
        oth[0]()
        own[4](0)
        own[3]()
        oth[1]()
        oth[2]()
        own[4](1)
        oth[4](0)
        own[4](2)
        oth[3]()
        oth[4](1)
        if last:
            for c in to_g1:
                c.wait_recv()
            total = pack[...]
            for n in range(7):
                total = total + gain_in[n]
            gain_in[7] = total
            to_g2 = [
                remote(gain_in.at[7], gain_z.at[n], m["s_g2"], n, **t) for n, t in enumerate(zmates)
            ]
            for c in to_g2:
                c.start()
        own[4](3)
        oth[4](2)
        if last:
            for c in to_g2:
                c.wait_recv()
            total = (gain_in[7] + gain_z[0] + gain_z[1] + gain_z[2]) * (1.0 / 4)
            gain_z[3] = total
            to_g3 = [
                remote(gain_z.at[3], gain_y.at[n], m["s_g3"], n, **t) for n, t in enumerate(ymates)
            ]
            for c in to_g3:
                c.start()
        oth[4](3)
        if last:
            finish_weights(0, to_xl[0])
            for c in to_g3:
                c.wait_recv()
            for n in range(-1, 3):
                ref = gain_z.at[3] if n < 0 else gain_y.at[n]
                yy = lax.rem(y + 3 - n, 4)
                for k in range(9):
                    at = pl.ds(pl.multiple_of(yy * CB + k * 128, 128), 128)
                    gain_out[1:2, at] = ref[k : k + 1, :]
                    gain_out[0:1, at] = ref[9 + k : 10 + k, :]
        for k in range(4):
            own[5](k)
            oth[5](k)

        for ring in (ring_a1, ring_b1, ring_a2, ring_b2):
            ring.drain()
        for c in (kv_pair[l], dkv_pair[l], to_x, across, *to_core, *to_stat):
            c.wait_send()
        own[6]()
        oth[6]()
    to_xl[0].wait_send()
    for c in (*to_g1, *to_g2, *to_g3):
        c.wait_send()


def step(lengths, reach, x, g, gain, wq, wk, wv, wo, cosine, sine):
    sem = pltpu.SemaphoreType.DMA
    hbm = pl.BlockSpec(memory_space=pl.ANY)
    vmem = pl.BlockSpec(memory_space=pltpu.VMEM)
    smem = pl.BlockSpec(memory_space=pltpu.SMEM)
    half = HD // 2
    scratch = dict(
        x=VMEM((2, 96, D), BF16),
        normed=VMEM((SEQ, D), BF16),
        g0=VMEM((SEQ, D), BF16),
        g1=VMEM((SEQ, D), BF16),
        S=VMEM((4, 2, RB, D), BF16),
        T=VMEM((SEQ, D), BF16),
        wkv=VMEM((HD, D), BF16),
        wq=VMEM((D, HD), BF16),
        wo=VMEM((HD, D), BF16),
        x_own=VMEM((LAYERS, RB, CB), BF16),
        recip=VMEM((LAYERS, SEQ, HD), F32),
        kv=VMEM((SEQ, HD), F32),
        kv_send=VMEM((LAYERS, SEQ, HD), BF16),
        kv_in=VMEM((LAYERS, SEQ, HD), BF16),
        q=VMEM((SEQ, HD), BF16),
        keep=VMEM((SEQ, HD), BF16),
        send=VMEM((LAYERS, SEQ, HD), BF16),
        dkv_in=VMEM((LAYERS, SEQ, HD), BF16),
        dkv=VMEM((SEQ, HD), BF16),
        dkv_t=VMEM((HD, SEQ), BF16),
        dq=VMEM((SEQ, HD), BF16),
        dq_t=VMEM((HD, SEQ), BF16),
        att_t=VMEM((HD, SEQ), BF16),
        a1=VMEM((8, 2, RB, CB), BF16),
        b1=VMEM((8, RB, 2 * CB), BF16),
        a2=VMEM((8, RB, CB), BF16),
        b2=VMEM((8, RB, CB), BF16),
        ua=VMEM((4, RB, CB), BF16),
        ub=VMEM((RB, D), BF16),
        va=VMEM((2, RB, CB), BF16),
        x_in=VMEM((RB, CB), BF16),
        stat_out=VMEM((LAYERS, RB, HD), F32),
        stat_in=VMEM((LAYERS, 3, RB, HD), F32),
        core_in=VMEM((LAYERS, 2, SEQ, CB), BF16),
        xl_out=VMEM((SEQ, CB), BF16),
        xl_in=VMEM((LAYERS, SEQ, CB), BF16),
        dw=VMEM((SEQ, CB), F32),
        pack=VMEM((24, 128), F32),
        gain_in=VMEM((8, 24, 128), F32),
        gain_z=VMEM((4, 24, 128), F32),
        gain_y=VMEM((3, 24, 128), F32),
        s_local=sem((32,)),
        s_kv=sem((LAYERS, 2, 1)),
        s_dkv=sem((LAYERS, 2, 1)),
        s_a1=sem((LAYERS, 2, 6)),
        s_b1=sem((LAYERS, 2, 6)),
        s_a2=sem((LAYERS, 2, 6)),
        s_b2=sem((LAYERS, 2, 6)),
        s_x=sem((LAYERS, 2, 1)),
        s_stat=sem((LAYERS, 2, 3)),
        s_core=sem((LAYERS, 2, 2)),
        s_xl=sem((LAYERS, 2, 1)),
        s_g1=sem((2, 7)),
        s_g2=sem((2, 3)),
        s_g3=sem((2, 3)),
        s_ag_x=sem((LAYERS, 2, 1)),
        s_ag=sem((LAYERS, 2, 32)),
    )
    return pl.pallas_call(
        step_kernel,
        in_specs=[smem, smem, hbm, hbm, vmem, hbm, hbm, hbm, hbm, vmem, vmem],
        out_specs=[vmem] * 6,
        out_shape=[
            jax.ShapeDtypeStruct((SEQ, D), BF16),
            jax.ShapeDtypeStruct((LAYERS, CB, HD), F32),
            jax.ShapeDtypeStruct((LAYERS, half, CB), F32),
            jax.ShapeDtypeStruct((LAYERS, half, CB), F32),
            jax.ShapeDtypeStruct((LAYERS, HD, CB), F32),
            jax.ShapeDtypeStruct((LAYERS, D), F32),
        ],
        scratch_shapes=[scratch],
        compiler_params=pltpu.CompilerParams(
            collective_id=0, has_side_effects=True, vmem_limit_bytes=VMEM_LIMIT
        ),
        name="step",
    )(lengths, reach, x, g, gain, wq, wk, wv, wo, cosine, sine)


def local(layer_inputs, out_grad, gain, w_query, w_key, w_value, w_out, doc_lengths, window_reach):
    cosine, sine = (jnp.asarray(t) for t in rope_tables())
    wk, wv = jnp.swapaxes(w_key, 1, 2), jnp.swapaxes(w_value, 1, 2)
    outs = step(
        doc_lengths, window_reach, layer_inputs, out_grad, gain, w_query, wk, wv, w_out, cosine, sine
    )
    g, dwq, dwk, dwv, dwo, dgain = write_out(*outs)
    return (g, dwq, jnp.swapaxes(dwk, 1, 2), jnp.swapaxes(dwv, 1, 2), dwo, dgain)


def solution(mesh):
    split = Mesh(mesh.devices.reshape(2, 2, 4, 2, 4), (XL, CORE, Y, XH, Z))
    in_specs = (
        P(None, DP, None),
        P(DP, None),
        P(),
        P(None, None, TP),
        P(None, None, TP),
        P(None, None, TP),
        P(None, TP, None),
        P(DP, None),
        P(),
    )
    out_specs = (
        P(DP, None),
        P(None, DP, TP),
        P(None, DP, TP),
        P(None, DP, TP),
        P(None, TP, DP),
        P(),
    )
    return jax.shard_map(local, mesh=split, in_specs=in_specs, out_specs=out_specs, check_vma=False)
```

time: 575 us -> 167 us (0.29); the launches traced: 564 us -> 167 us
  waiting for transfers between devices: 304 us -> 0 us
  Pallas kernels: 0 us -> 159 us
  matrix products: 78.5 us -> 0 us
  blocking collectives: 54.7 us -> 0 us
  local copies, waits for them, and re-layouts: 54.9 us -> 7.43 us
  starting transfers between devices: 27.8 us -> 0 us
  other arithmetic: 27.1 us -> 0 us
  between operations: 16.7 us -> 0.66 us
    pallas_call x0 -> x2, Pallas kernels: none -> 159 us  [the longest x1 156 us: step(): pl.pallas_call(step_kernel, in_specs=[smem, smem, hbm, hbm, vmem, hbm, hb...]
    unnamed x10 -> x0, waiting for transfers between devices: 89.6 us -> none
    dot_general x42 -> x0, matrix products: 78.5 us -> none  [the longest x12 38.7 us: contract_rows(): lax.dot_general(left_side, right_side, (((0,), (0,)), ((), ())), preferre...]
    all_to_all x4 -> x0, waiting for transfers between devices: 76.6 us -> none  [sum_at_owner(): lax.all_to_all(pieces, axis, split_axis=0, concat_axis=0, tiled=True)]
    all_gather x2 -> x0, waiting for transfers between devices: 73.8 us -> none  [local(): full_upstream = lax.all_gather(local_layer, TP, axis=0, tiled=True)]
    reduce_scatter x4 -> x0, waiting for transfers between devices: 61.8 us -> none  [sum_in_order(): pieces = lax.psum_scatter(pieces, axes[k], scatter_dimension=0, tiled=True)]
    psum x5 -> x0, blocking collectives: 54.7 us -> none  [by_axis(): return functools.reduce(lax.psum, axes, x)]
    unnamed x171 -> x12, local copies, waits for them, and re-layouts: 24.5 us -> 7.43 us
  transfers between devices with their start and end apart: 20 -> 0, of which waited for: 11 -> 0; matrix products, arithmetic and copies ran while one was open for 18% -> 0% of each run, Pallas kernels for 0% -> 0%
where the time goes in v2:
time: 167 us
  Pallas kernels  159 us (95%)
  local copies, waits for them, and re-layouts  7.43 us (4%)
    pallas_call x1, Pallas kernels, step(): pl.pallas_call(step_kernel, in_specs=[smem, smem, hbm, hbm, vmem, hbm, hb...  156 us
    unnamed x12, local copies, waits for them, and re-layouts  7.43 us

profile of v2, /device:TPU:0, one launch (start us, length us, event | category | flops | bytes accessed | tf_op | source)
XLA Modules:
  0.0 167.0 jit_solution(6046162099420722765)
XLA Ops:
  0.6 156.0 %step.1 = (bf16[384,4608]{1,0:T(8,128)(2,1)}, f32[2,1152,128]{2,1,0:T(8,128)}, f32[2,64,1152]{2,1,0:T(8,128)}, f32[2,64,1152]{2,1,0:T(8,128)}, f32[2,128,1152]{2,1,0:T(8,128)}, /*index=5*/f32[2,4608]{1,0:T(2,128)}) custom-call(s32[1,4]{1,0:T(1,128)} %lengths.1, s32[2]{0:T(128)} %reach.1, bf16[2,384,4608]{2,1,0:T(8,128)(2,1)} %x_hbm.1, ...), custom_call_target="tpu_custom_call" | custom-call | tf_op jit(solution)/shard_map/step/pallas_call | solution.py:703
  156.6 0.0 copy-start
  156.6 2.0 %copy-done = bf16[384,4608]{1,0:T(8,128)(2,1)S(1)} copy-done((bf16[384,4608]{1,0:T(8,128)(2,1)S(1)}, bf16[384,4608]{1,0:T(8,128)(2,1)}, u32[]{:S(2)}) %copy-start) | copy-done | bytes 3538968
  158.6 0.0 copy-start.1
  158.6 1.3 copy-done.1
  159.9 0.0 copy-start.2
  159.9 1.3 copy-done.2
  161.2 0.0 copy-start.3
  161.2 1.1 copy-done.3
  162.2 0.0 copy-start.4
  162.2 1.1 copy-done.4
  163.3 0.0 copy-start.5
  163.3 0.8 copy-done.5
  164.1 3.0 %write_out.1 = (bf16[384,4608]{1,0:T(8,128)(2,1)}, f32[2,1152,128]{2,1,0:T(8,128)}, f32[2,64,1152]{2,1,0:T(8,128)}, f32[2,64,1152]{2,1,0:T(8,128)}, f32[2,128,1152]{2,1,0:T(8,128)}, /*index=5*/f32[2,4608]{1,0:T(2,128)}) custom-call(bf16[384,4608]{1,0:T(8,128)(2,1)S(1)} %copy-done, f32[2,1152,128]{2,1,0:T(8,128)S(1)} %copy-done.1, ...), custom_call_target="tpu_custom_call" | custom-call | tf_op jit(solution)/shard_map/write_out/pallas_call | solution.py:135
Async XLA Ops:
  156.6 2.0 %copy-start = (bf16[384,4608]{1,0:T(8,128)(2,1)S(1)}, bf16[384,4608]{1,0:T(8,128)(2,1)}, u32[]{:S(2)}) copy-start(bf16[384,4608]{1,0:T(8,128)(2,1)} %get-tuple-element.18.refs_0_) | copy-start | bytes 10616836
  158.6 1.3 copy-start.1
  159.9 1.3 copy-start.2
  161.2 1.1 copy-start.3
  162.2 1.1 copy-start.4
  163.3 0.8 copy-start.5

commit v3 on v2

--- a/solution.py
+++ b/solution.py
@@ -68,52 +68,48 @@
 
 
 class Ring:
-    def __init__(self, axis, src, bufs, ss, rs):
+    def __init__(self, axis, src, buf, sems, out):
         i = lax.axis_index(axis)
         up, dn, far = lax.rem(i + 1, 4), lax.rem(i + 3, 4), lax.rem(i + 2, 4)
-        r1p, r1m, r2p, r2m, r3p, r3m, tp, tm = bufs
+        low, high = pl.ds(0, CA), pl.ds(CA, CB - CA)
+        self.first = buf.at[0, :, low], buf.at[0, :, high]
+        self.turned = buf.at[3, :, low], buf.at[3, :, high]
+        self.direct, self.summed = buf.at[1], buf.at[2]
         plan = [
-            (src(far, 0), r1p, up),
-            (src(far, 1), r1m, dn),
-            (src(up, 1), r2p, up),
-            (src(dn, 0), r2m, dn),
-            (tp, r3p, up),
-            (tm, r3m, dn),
+            (src(far, 0), self.first[0], up),
+            (src(far, 1), self.first[1], dn),
+            (src(up, 1), buf.at[1, :, high], up),
+            (src(dn, 0), buf.at[1, :, low], dn),
+            (self.turned[0], buf.at[2, :, low], up),
+            (self.turned[1], buf.at[2, :, high], dn),
         ]
         self.copies = [
             pltpu.make_async_remote_copy(
                 src_ref=s,
                 dst_ref=d,
-                send_sem=ss.at[n],
-                recv_sem=rs.at[n],
+                send_sem=sems.at[0, n],
+                recv_sem=sems.at[1, n],
                 device_id={axis: to},
                 device_id_type=MESH,
             )
             for n, (s, d, to) in enumerate(plan)
         ]
-        self.i, self.up, self.dn, self.src, self.bufs = i, up, dn, src, bufs
-
-    def start(self, which):
+        self.i, self.sides, self.src, self.out = i, (up, dn), src, out
+
+    def start(self, *which):
         for n in which:
             self.copies[n].start()
 
-    def middle(self):
-        r1p, r1m, _, _, _, _, tp, tm = self.bufs
-        self.copies[0].wait_recv()
-        tp[...] = add(r1p, self.src(self.up, 0)).astype(BF16)
-        self.copies[4].start()
-        self.copies[1].wait_recv()
-        tm[...] = add(r1m, self.src(self.dn, 1)).astype(BF16)
-        self.copies[5].start()
-
-    def finish(self, out):
-        _, _, r2p, r2m, r3p, r3m, _, _ = self.bufs
-        self.copies[3].wait_recv()
-        self.copies[4].wait_recv()
-        out(0)[...] = add(self.src(self.i, 0), r3p, r2m).astype(BF16)
-        self.copies[2].wait_recv()
-        self.copies[5].wait_recv()
-        out(1)[...] = add(self.src(self.i, 1), r2p, r3m).astype(BF16)
+    def middle(self, *which):
+        for h in which:
+            self.copies[h].wait_recv()
+            self.turned[h][...] = add(self.first[h], self.src(self.sides[h], h)).astype(BF16)
+            self.copies[4 + h].start()
+
+    def finish(self):
+        for n in range(2, 6):
+            self.copies[n].wait_recv()
+        self.out[...] = add(self.src(self.i, None), self.direct, self.summed).astype(BF16)
 
     def drain(self):
         for c in self.copies:
@@ -222,41 +218,50 @@
     kv_pair = [remote(m["kv_send"].at[l], m["kv_in"].at[l], m["s_kv"].at[l], 0, **pair) for l in (0, 1)]
     cs, sn = cosine, sine
 
-    def front(l):
+    def front_norm(l, c):
         x, normed = m["x"], m["normed"]
-        for c in range(4):
-            get_x[l][c].wait()
-
-            @pl.loop(0, 6)
-            def _(r):
-                at = pl.ds(pl.multiple_of(c * 96 + r * 16, 16), 16)
-                v = x[c % 2, pl.ds(pl.multiple_of(r * 16, 16), 16), :].astype(F32)
-                rc = lax.rsqrt(jnp.sum(v * v, axis=1, keepdims=True) * (1.0 / D) + epsilon)
-                normed[at, :] = (v * rc * gain[l : l + 1, :]).astype(BF16)
-                m["recip"][l, at, :] = jnp.broadcast_to(rc, (16, HD))
-
-            if c < 2:
-                get_x[l][c + 2].start()
-            elif l == 1:
-                get_x[0][c - 2].start()
-
+        get_x[l][c].wait()
+
+        @pl.loop(0, 2)
+        def _(r):
+            at = pl.ds(pl.multiple_of(c * 96 + r * RB, 16), RB)
+            there = pl.ds(pl.multiple_of(r * RB, 16), RB)
+            squares = jnp.zeros((RB, HD), F32)
+            for k in range(D // HD):
+                col = slice(k * HD, (k + 1) * HD)
+                v = x[c % 2, there, col].astype(F32)
+                squares = squares + v * v
+                normed[at, col] = (v * gain[l : l + 1, col]).astype(BF16)
+            m["squares"][at, :] = squares
+
+        if c < 2:
+            get_x[l][c + 2].start()
+        elif l == 1:
+            get_x[0][c - 2].start()
+
+    def front_kv(l):
+        rc = jnp.sum(m["squares"][...], axis=1, keepdims=True) * (1.0 / D)
+        m["recip"][l] = jnp.broadcast_to(lax.rsqrt(rc + epsilon), (SEQ, HD))
         for c in get_wkv[l]:
             c.wait()
         acc = jnp.zeros((SEQ, HD), F32)
         for c in range(3):
             at = slice(c * 1536, (c + 1) * 1536)
-            acc = acc + dot_nt(normed[:, at], m["wkv"][:, at])
+            acc = acc + dot_nt(m["normed"][:, at], m["wkv"][:, at])
+        acc = acc * m["recip"][l]
         m["kv"][...] = acc
         m["kv_send"][l] = acc.astype(BF16)
         if l == 1:
             pl.semaphore_wait(barrier, 13)
         kv_pair[l].start()
+
+    def front_q(l):
         get_wq[l].wait()
         acc = jnp.zeros((SEQ, HD), F32)
         for c in range(3):
             at = slice(c * 1536, (c + 1) * 1536)
-            acc = acc + dot_nn(normed[:, at], m["wq"][at, :])
-        m["q"][...] = rotate(acc, cs[...], sn[...]).astype(BF16)
+            acc = acc + dot_nn(m["normed"][:, at], m["wq"][at, :])
+        m["q"][...] = rotate(acc * m["recip"][l], cs[...], sn[...]).astype(BF16)
 
     low = lax.broadcasted_iota(jnp.int32, (SEQ, HD), 1) < half
 
@@ -306,31 +311,61 @@
         delta = jnp.sum(ga.astype(F32) * att.astype(F32), axis=1, keepdims=True)
         ds = prob * (dot_nt(ga, v) - delta) * (1.0 - squashed * squashed) * score_scale
         ds = ds.astype(BF16)
-        dk = unrotate(dot_tn(ds, q), cs[...], sn[...])
+        dk_turned = dot_tn(ds, q)
         dv = dot_tn(rounded, ga)
+        dk = unrotate(dk_turned, cs[...], sn[...])
         lower = jnp.where(low, dk, pltpu.roll(dv, half, 1))
         upper = jnp.where(low, pltpu.roll(dk, half, 1), dv)
         m["keep"][...] = jnp.where(even, lower, upper).astype(BF16)
         m["send"][l] = jnp.where(even, upper, lower).astype(BF16)
         dkv_pair[l].start()
-        dq = unrotate(dot_nn(ds, k), cs[...], sn[...]).astype(BF16)
-        m["dq"][...] = dq
-        m["dq_t"][...] = dq.T
+        dq_turned = dot_nn(ds, k)
+        stat = dq_turned * q.astype(F32) + dk_turned * k.astype(F32) + dv * v.astype(F32)
+        stat = jnp.sum(stat, axis=1, keepdims=True)
+        m["stat_out"][l, 0] = jnp.broadcast_to(stat, (SEQ, HD)).T[:8]
+        for c in stat_y[l]:
+            c.start()
+        dq = unrotate(dq_turned, cs[...], sn[...])
+        m["dq"][...] = dq.astype(BF16)
+        m["dqkv_t"][:HD] = (dq * m["recip"][l]).astype(BF16).T
         m["att_t"][...] = att.T
 
+    stat_y, stat_z, stat_x = (
+        [
+            [
+                remote(
+                    m["stat_out"].at[l, step],
+                    m["stat_in"].at[l, 3 * step + n],
+                    m["s_stat"].at[l],
+                    3 * step + n,
+                    **t,
+                )
+                for n, t in enumerate(mates)
+            ]
+            for l in (0, 1)
+        ]
+        for step, mates in enumerate((ymates, zmates, [{XH: 1 - xh}]))
+    )
+
+    def stat_sum(l, step, copies):
+        for c in copies:
+            c.wait_recv()
+        total = m["stat_out"][l, step]
+        for n in range(len(copies)):
+            total = total + m["stat_in"][l, 3 * step + n]
+        return total
+
     dkv_pair = [remote(m["send"].at[l], m["dkv_in"].at[l], m["s_dkv"].at[l], 0, **pair) for l in (0, 1)]
 
     S, T = m["S"], m["T"]
-    part = [pl.ds(0, CA), pl.ds(CA, CB - CA)]
-    kinds = (0, 1, 1, 0, 0, 1, 0, 1)
 
     def dp_cols(k):
         return pl.ds(pl.multiple_of((2 * k + core) * CB, 128), CB)
 
-    def finish_weights(l, to_xl):
-        to_xl.wait_recv()
-
-        @pl.loop(0, 9)
+    def finish_weights(l, quarter):
+        cuts = (0, 3, 5, 7, 9)
+
+        @pl.loop(cuts[quarter], cuts[quarter + 1])
         def _(k):
             at = pl.ds(pl.multiple_of(k * 128, 128), 128)
             v = (m["dw"][:, at] + m["xl_in"][l, :, at].astype(F32)) * (1.0 / 4)
@@ -339,7 +374,10 @@
             dwv[l, :, at] = v[HD + half : 2 * HD]
             dwo[l, :, at] = v[2 * HD :]
 
-    front(1)
+    for c in range(4):
+        front_norm(1, c)
+    front_kv(1)
+    front_q(1)
     pack = m["pack"]
     pack[...] = jnp.zeros((24, 128), F32)
     to_xl = {}
@@ -355,46 +393,35 @@
         @pl.loop(0, D // 512)
         def _(c):
             at = pl.ds(pl.multiple_of(c * 512, 512), 512)
-            T[:HD, at] = dot_nn(m["dq_t"][...], normed[:, at]).astype(BF16)
             T[2 * HD :, at] = dot_nn(m["att_t"][...], g[:, at]).astype(BF16)
 
         dkv_pair[l].wait_recv()
-        dkv = add(m["keep"], m["dkv_in"].at[l]).astype(BF16)
-        m["dkv"][...] = dkv
-        m["dkv_t"][...] = dkv.T
-
-        sa1, sb1, sa2, sb2 = (m[n].at[l] for n in ("s_a1", "s_b1", "s_a2", "s_b2"))
+        dkv = add(m["keep"], m["dkv_in"].at[l])
+        m["dkv"][...] = dkv.astype(BF16)
+        m["dqkv_t"][HD:] = (dkv * m["recip"][l]).astype(BF16).T
+        m["stat_out"][l, 1] = stat_sum(l, 0, stat_y[l])
+        for c in stat_z[l]:
+            c.start()
+
         ua, ub, va = m["ua"], m["ub"], m["va"]
-        ring_a1 = Ring(
-            Y,
-            lambda t, h: S.at[pl.ds(2 * h, 2), 0, :, cols(t)],
-            [m["a1"].at[n] for n in range(8)],
-            sa1.at[0],
-            sa1.at[1],
-        )
-        ring_b1 = Ring(
-            Z,
-            lambda t, h: S.at[t, 1, :, pl.ds(h * 2 * CB, 2 * CB)],
-            [m["b1"].at[n] for n in range(8)],
-            sb1.at[0],
-            sb1.at[1],
-        )
-        ring_a2 = Ring(
-            Z,
-            lambda t, h: ua.at[t, :, part[h]],
-            [m["a2"].at[n, :, part[h]] for n, h in enumerate(kinds)],
-            sa2.at[0],
-            sa2.at[1],
-        )
-        ring_b2 = Ring(
-            Y,
-            lambda t, h: ub.at[:, cols(t, (CA, CB - CA)[h], h * CA)],
-            [m["b2"].at[n, :, part[h]] for n, h in enumerate(kinds)],
-            sb2.at[0],
-            sb2.at[1],
-        )
-
-        for k, starts in ((2, (0, 1)), (1, (2,)), (3, (3,)), (0, ())):
+        spans = ((0, CA), (CA, CB - CA), (0, CB))
+        ring_a, ring_b = {}, {}
+
+        def sub(t, h):
+            shift, width = spans[2 if h is None else h]
+            return cols(t, width, shift)
+
+        def ring(n, axis, src, out):
+            return Ring(axis, src, m["ring"].at[n], m["s_ring"].at[l, n], out)
+
+        for n, k in enumerate((2, 1, 3, 0)):
+            zk, yk = lax.rem(z + k, 4), lax.rem(y + k, 4)
+            ring_a[k] = ring(n, Y, lambda t, h, zk=zk: S.at[zk, 0, :, sub(t, h)], ua.at[zk])
+            ring_b[k] = ring(4 + n, Z, lambda t, h, yk=yk: S.at[t, 1, :, sub(yk, h)], ub.at[yk])
+        a2 = ring(8, Z, lambda t, h: ua.at[t, :, pl.ds(*spans[2 if h is None else h])], va.at[0])
+        b2 = ring(9, Y, lambda t, h: ub.at[t, :, pl.ds(*spans[2 if h is None else h])], va.at[1])
+
+        for k in (2, 1, 3, 0):
 
             @pl.loop(0, 3)
             def _(c):
@@ -403,8 +430,10 @@
                 v = v + dot_nn(m["dkv"][...], m["wkv"][:, at])
                 S[:, :, :, at] = v.astype(BF16).reshape(4, 2, RB, 384)
 
-            ring_a1.start(starts)
-        ring_b1.start(range(4))
+            if k in (2, 1):
+                ring_b[k].start(0, 1, 2, 3)
+        ring_a[2].start(0, 1, 2, 3)
+        ring_a[1].start(0, 1, 2, 3)
         if not last:
             for c in (*get_wkv[0], get_wq[0]):
                 c.start()
@@ -412,7 +441,7 @@
         @pl.loop(0, D // 512)
         def _(c):
             at = pl.ds(pl.multiple_of(c * 512, 512), 512)
-            T[HD : 2 * HD, at] = dot_nn(m["dkv_t"][...], normed[:, at]).astype(BF16)
+            T[: 2 * HD, at] = dot_nn(m["dqkv_t"][...], normed[:, at]).astype(BF16)
 
         to_core = [
             remote(
@@ -427,22 +456,43 @@
         to_core[0].start()
         to_core[1].start()
 
-        ring_a1.middle()
-        ring_b1.middle()
+        def aside(c):
+            if last:
+                finish_weights(1, c)
+            else:
+                front_norm(0, c)
+
+        def both(do):
+            do(ring_b, b2)
+            do(ring_a, a2)
+
+        both(lambda r, _: r[2].middle(0, 1))
+        both(lambda r, _: r[3].start(0, 1, 2, 3))
+        both(lambda r, _: r[1].middle(0, 1))
+        both(lambda r, _: r[0].start(0, 1, 2, 3))
         if last:
-            finish_weights(1, to_xl[1])
-        else:
-            front(0)
-        ring_a1.finish(lambda h: ua.at[pl.ds(2 * h, 2)])
-        ring_a2.start(range(4))
-        ring_b1.finish(lambda h: ub.at[:, pl.ds(h * 2 * CB, 2 * CB)])
-        ring_b2.start(range(4))
-        ring_a2.middle()
-        ring_b2.middle()
-        ring_a2.finish(lambda h: va.at[0, :, part[h]])
-        ring_b2.finish(lambda h: va.at[1, :, part[h]])
+            to_xl[1].wait_recv()
+        aside(0)
+        both(lambda r, r2: (r[2].finish(), r2.start(0, 1)))
+        m["stat_out"][l, 2] = stat_sum(l, 1, stat_z[l])
+        stat_x[l][0].start()
+        both(lambda r, _: r[3].middle(0, 1))
+        aside(1)
+        both(lambda r, r2: (r[1].finish(), r2.start(2)))
+        both(lambda r, _: r[0].middle(0, 1))
+        aside(2)
+        both(lambda r, r2: (r[3].finish(), r2.start(3)))
+        both(lambda _, r2: r2.middle(0))
+        both(lambda _, r2: r2.middle(1))
+        aside(3)
+        both(lambda r, r2: (r[0].finish(), r2.finish()))
         to_x = remote(va.at[1 - xh], m["x_in"], m["s_x"].at[l], 0, **{XH: 1 - xh})
         to_x.start()
+        if not last:
+            front_kv(0)
+
+        total = stat_sum(l, 2, stat_x[l])
+        m["stat"][...] = jnp.broadcast_to(total[:1], (HD, SEQ)).T
 
         for c in to_core:
             c.wait_recv()
@@ -464,14 +514,6 @@
         gn = gain[l : l + 1, cols(y)]
         unit = m["x_own"][l].astype(F32) * rc
         u = grad * gn
-        stat = jnp.sum(u * unit, axis=1, keepdims=True)
-        m["stat_out"][l] = jnp.broadcast_to(stat, (RB, HD))
-        to_stat = [
-            remote(m["stat_out"].at[l], m["stat_in"].at[l, n], m["s_stat"].at[l], n, **t)
-            for n, t in enumerate(ymates)
-        ]
-        for c in to_stat:
-            c.start()
         per_feature = jnp.sum(grad * unit, axis=0, keepdims=True)
         for n in range(9):
             k = n + 9 if last else n
@@ -483,12 +525,7 @@
             ]
             for c in to_g1:
                 c.start()
-        for c in to_stat:
-            c.wait_recv()
-        total = m["stat_out"][l]
-        for n in range(3):
-            total = total + m["stat_in"][l, n]
-        mean = total[:, :1] * (1.0 / D)
+        mean = m["stat"][rows, :][:, :1] * (1.0 / D)
         up_own = g[rows, cols(y)].astype(F32)
         to[rows, cols(y)] = (up_own + rc * (u - unit * mean)).astype(BF16)
 
@@ -523,20 +560,18 @@
             def arrive_dn():
                 one(order[1], j, 0, up1).wait_recv()
                 go(one(order[1], j, 2, up1, 0, CA))
-                go(one(order[1], j, 6, up2))
-                go(one(order[1], j, 7, dn2))
 
             def arrive_up():
                 one(order[2], j, 1, dn1).wait_recv()
                 go(one(order[2], j, 3, dn1, CA, CB - CA))
-                go(one(order[2], j, 8, up2))
-                go(one(order[2], j, 9, dn2))
 
             def arrive_far():
                 one(order[3], j, 2, up1, 0, CA).wait_recv()
                 one(order[3], j, 3, dn1, CA, CB - CA).wait_recv()
-                go(one(order[3], j, 10, up2))
-                go(one(order[3], j, 11, dn2))
+
+            def across(k):
+                go(one(order[k], j, 4 + 2 * k, up2))
+                go(one(order[k], j, 5 + 2 * k, dn2))
 
             def second_step(k):
                 one(order[k], jdn, 4 + 2 * k, up2).wait_recv()
@@ -553,7 +588,7 @@
                 for c in sent:
                     c.wait_send()
 
-            return begin, arrive_dn, arrive_up, arrive_far, second_step, last_step, done
+            return begin, arrive_dn, arrive_up, arrive_far, second_step, last_step, done, across
 
         mine = to.at[rows, cols(y)]
         across = remote(mine, mine, m["s_ag_x"].at[l], 0, **{XH: 1 - xh})
@@ -571,18 +606,26 @@
             m["dw"][at, :] = here
 
         own[1]()
+        own[7](1)
         own[2]()
         theirs = to.at[rows_of(z, 1 - xh), cols(y)]
         remote(theirs, theirs, m["s_ag_x"].at[l], 0, **{XH: 1 - xh}).wait_recv()
         oth[0]()
+        own[7](2)
+        if not last:
+            front_q(0)
+        oth[1]()
+        oth[7](1)
+        oth[2]()
+        oth[7](2)
+        own[3]()
+        own[7](3)
         own[4](0)
-        own[3]()
-        oth[1]()
-        oth[2]()
+        oth[3]()
+        oth[7](3)
         own[4](1)
         oth[4](0)
         own[4](2)
-        oth[3]()
         oth[4](1)
         if last:
             for c in to_g1:
@@ -610,7 +653,9 @@
                 c.start()
         oth[4](3)
         if last:
-            finish_weights(0, to_xl[0])
+            to_xl[0].wait_recv()
+            for c in range(4):
+                finish_weights(0, c)
             for c in to_g3:
                 c.wait_recv()
             for n in range(-1, 3):
@@ -624,9 +669,9 @@
             own[5](k)
             oth[5](k)
 
-        for ring in (ring_a1, ring_b1, ring_a2, ring_b2):
-            ring.drain()
-        for c in (kv_pair[l], dkv_pair[l], to_x, across, *to_core, *to_stat):
+        for r in (*ring_a.values(), *ring_b.values(), a2, b2):
+            r.drain()
+        for c in (kv_pair[l], dkv_pair[l], to_x, across, *to_core, *stat_y[l], *stat_z[l], *stat_x[l]):
             c.wait_send()
         own[6]()
         oth[6]()
@@ -661,20 +706,18 @@
         send=VMEM((LAYERS, SEQ, HD), BF16),
         dkv_in=VMEM((LAYERS, SEQ, HD), BF16),
         dkv=VMEM((SEQ, HD), BF16),
-        dkv_t=VMEM((HD, SEQ), BF16),
+        dqkv_t=VMEM((2 * HD, SEQ), BF16),
         dq=VMEM((SEQ, HD), BF16),
-        dq_t=VMEM((HD, SEQ), BF16),
         att_t=VMEM((HD, SEQ), BF16),
-        a1=VMEM((8, 2, RB, CB), BF16),
-        b1=VMEM((8, RB, 2 * CB), BF16),
-        a2=VMEM((8, RB, CB), BF16),
-        b2=VMEM((8, RB, CB), BF16),
+        ring=VMEM((10, 4, RB, CB), BF16),
         ua=VMEM((4, RB, CB), BF16),
-        ub=VMEM((RB, D), BF16),
+        ub=VMEM((4, RB, CB), BF16),
         va=VMEM((2, RB, CB), BF16),
         x_in=VMEM((RB, CB), BF16),
-        stat_out=VMEM((LAYERS, RB, HD), F32),
-        stat_in=VMEM((LAYERS, 3, RB, HD), F32),
+        squares=VMEM((SEQ, HD), F32),
+        stat=VMEM((SEQ, HD), F32),
+        stat_out=VMEM((LAYERS, 3, 8, SEQ), F32),
+        stat_in=VMEM((LAYERS, 7, 8, SEQ), F32),
         core_in=VMEM((LAYERS, 2, SEQ, CB), BF16),
         xl_out=VMEM((SEQ, CB), BF16),
         xl_in=VMEM((LAYERS, SEQ, CB), BF16),
@@ -686,12 +729,9 @@
         s_local=sem((32,)),
         s_kv=sem((LAYERS, 2, 1)),
         s_dkv=sem((LAYERS, 2, 1)),
-        s_a1=sem((LAYERS, 2, 6)),
-        s_b1=sem((LAYERS, 2, 6)),
-        s_a2=sem((LAYERS, 2, 6)),
-        s_b2=sem((LAYERS, 2, 6)),
+        s_ring=sem((LAYERS, 10, 2, 6)),
         s_x=sem((LAYERS, 2, 1)),
-        s_stat=sem((LAYERS, 2, 3)),
+        s_stat=sem((LAYERS, 2, 7)),
         s_core=sem((LAYERS, 2, 2)),
         s_xl=sem((LAYERS, 2, 1)),
         s_g1=sem((2, 7)),
@@ -705,12 +745,12 @@
         in_specs=[smem, smem, hbm, hbm, vmem, hbm, hbm, hbm, hbm, vmem, vmem],
         out_specs=[vmem] * 6,
         out_shape=[
-            jax.ShapeDtypeStruct((SEQ, D), BF16),
-            jax.ShapeDtypeStruct((LAYERS, CB, HD), F32),
-            jax.ShapeDtypeStruct((LAYERS, half, CB), F32),
-            jax.ShapeDtypeStruct((LAYERS, half, CB), F32),
-            jax.ShapeDtypeStruct((LAYERS, HD, CB), F32),
-            jax.ShapeDtypeStruct((LAYERS, D), F32),
+            VMEM((SEQ, D), BF16),
+            VMEM((LAYERS, CB, HD), F32),
+            VMEM((LAYERS, half, CB), F32),
+            VMEM((LAYERS, half, CB), F32),
+            VMEM((LAYERS, HD, CB), F32),
+            VMEM((LAYERS, D), F32),
         ],
         scratch_shapes=[scratch],
         compiler_params=pltpu.CompilerParams(

time: 167 us -> 145 us (0.87)
  Pallas kernels: 159 us -> 144 us
  local copies, waits for them, and re-layouts: 7.43 us -> 0 us
    pallas_call x1, Pallas kernels: 156 us -> 141 us  [step(): pl.pallas_call(step_kernel, in_specs=[smem, smem, hbm, hbm, vmem, hbm, hb...]
    unnamed x12 -> x0, local copies, waits for them, and re-layouts: 7.43 us -> none
where the time goes in v3:
time: 145 us
  Pallas kernels  144 us (99%)
    pallas_call x1, Pallas kernels, step(): pl.pallas_call(step_kernel, in_specs=[smem, smem, hbm, hbm, vmem, hbm, hb...  141 us
    pallas_call x1, Pallas kernels, write_out(): pl.pallas_call(write_kernel, in_specs=[pl.BlockSpec(memory_space=pltpu.VM...  2.98 us

profile of v3, /device:TPU:0, one launch (start us, length us, event | category | flops | bytes accessed | tf_op | source)
XLA Modules:
  0.0 145.1 jit_solution(12934119404376325765)
XLA Ops:
  0.6 141.4 %step.1 = (bf16[384,4608]{1,0:T(8,128)(2,1)S(1)}, f32[2,1152,128]{2,1,0:T(8,128)S(1)}, f32[2,64,1152]{2,1,0:T(8,128)S(1)}, f32[2,64,1152]{2,1,0:T(8,128)S(1)}, f...) custom-call(s32[1,4]{1,0:T(1,128)} %lengths.1, s32[2]{0:T(128)} %reach.1, bf16[2,384,4608]{2,1,0:T(8,128)(2,1)} %x_hbm.1, ...), custom_call_target="tpu_custom_call" | custom-call | tf_op jit(solution)/shard_map/step/pallas_call | solution.py:743
  142.0 3.0 %write_out.1 = (bf16[384,4608]{1,0:T(8,128)(2,1)}, f32[2,1152,128]{2,1,0:T(8,128)}, f32[2,64,1152]{2,1,0:T(8,128)}, f32[2,64,1152]{2,1,0:T(8,128)}, f32[2,128,1152]{2,1,0:T(8,128)}, /*index=5*/f32[2,4608]{1,0:T(2,128)}) custom-call(bf16[384,4608]{1,0:T(8,128)(2,1)S(1)} %get-tuple-element.18.refs_0_, f32[2,1152,128]{2,1,0:T(8,128)S(1)} %get-tuple-element.19.refs_1_, ...), custom_call_target="tpu_custom_call" | custom-call | tf_op jit(solution)/shard_map/write_out/pallas_call | solution.py:131

commit v4 on v3

--- a/solution.py
+++ b/solution.py
@@ -116,10 +116,26 @@
             c.wait_send()
 
 
+class Fetch:
+    def __init__(self, src, dst, sem, pieces, second=False):
+        size = dst.shape[1 if second else 0] // pieces
+        at = [(slice(None),) * second + (pl.ds(k * size, size),) for k in range(pieces)]
+        self.parts = [pltpu.make_async_copy(src.at[i], dst.at[i], sem) for i in at]
+        self.whole = pltpu.make_async_copy(src, dst, sem)
+
+    def start(self):
+        for c in self.parts:
+            c.start()
+
+    def wait(self):
+        self.whole.wait()
+
+
 def write_kernel(*refs):
     *refs, sems = refs
     n = len(refs) // 2
-    copies = [pltpu.make_async_copy(refs[k], refs[n + k], sems.at[k]) for k in range(n)]
+    pieces = (12, 4, 2, 2, 4, 1)
+    copies = [Fetch(refs[k], refs[n + k], sems.at[k], pieces[k], k and k < 5) for k in range(n)]
     for c in copies:
         c.start()
     for c in copies:
@@ -190,26 +206,28 @@
     pair = {Z: z + 1 - 2 * lax.rem(z, 2)}
     even = lax.rem(z, 2) == 0
 
-    def fetch(n, src, dst):
-        return pltpu.make_async_copy(src, dst, m["s_local"].at[n])
+    def fetch(n, src, dst, pieces=1):
+        return Fetch(src, dst, m["s_local"].at[n], pieces)
 
     get_x, get_wkv, get_wq, get_wo, get_own = {}, {}, {}, {}, {}
     for l in (1, 0):
         get_x[l] = [
-            fetch(16 * l + c, x_hbm.at[l, pl.ds(c * 96, 96)], m["x"].at[c % 2])
+            fetch(16 * l + c, x_hbm.at[l, pl.ds(c * 96, 96)], m["x"].at[c % 2], 6)
             for c in range(4)
         ]
         get_wkv[l] = [
-            fetch(16 * l + 4, wk_hbm.at[l], m["wkv"].at[pl.ds(0, half)]),
-            fetch(16 * l + 5, wv_hbm.at[l], m["wkv"].at[pl.ds(half, half)]),
+            fetch(16 * l + 4, wk_hbm.at[l], m["wkv"].at[pl.ds(0, half)], 4),
+            fetch(16 * l + 5, wv_hbm.at[l], m["wkv"].at[pl.ds(half, half)], 4),
         ]
-        get_wq[l] = fetch(16 * l + 6, wq_hbm.at[l], m["wq"])
-        get_wo[l] = fetch(16 * l + 7, wo_hbm.at[l], m["wo"])
-        get_own[l] = fetch(16 * l + 8, x_hbm.at[l, rows_of(z, xh), cols(y)], m["x_own"].at[l])
-    get_g = fetch(9, g_hbm, m["g0"])
-    for c in (*get_x[1][:2], *get_wkv[1], get_wq[1], get_wo[1], get_g, get_own[1]):
+        get_wq[l] = fetch(16 * l + 6, wq_hbm.at[l], m["wq"], 8)
+        get_wo[l] = fetch(16 * l + 7, wo_hbm.at[l], m["wo"], 8)
+        get_own[l] = [
+            fetch(16 * l + 10 + n, x_hbm.at[l, rows_of(z, hh), cols(y)], m["x_own"].at[l, n])
+            for n, hh in enumerate((xh, 1 - xh))
+        ]
+    get_g = fetch(9, g_hbm, m["g0"], 12)
+    for c in (*get_x[1][:2], *get_wkv[1], get_wq[1], get_wo[1], get_g, *get_own[1], *get_own[0]):
         c.start()
-    get_own[0].start()
 
     barrier = pltpu.get_barrier_semaphore()
     for to in (*ymates, *zmates, *xmates):
@@ -265,7 +283,7 @@
 
     low = lax.broadcasted_iota(jnp.int32, (SEQ, HD), 1) < half
 
-    def attention(l, g):
+    def attention_upstream(l, g):
         if l == 1:
             get_g.wait()
         get_wo[l].wait()
@@ -273,8 +291,9 @@
         for c in range(3):
             at = slice(c * 1536, (c + 1) * 1536)
             ga = ga + dot_nt(g[:, at], m["wo"][:, at])
-        ga = ga.astype(BF16)
-
+        m["ga"][...] = ga.astype(BF16)
+
+    def attention_forward(l):
         kv_pair[l].wait_recv()
         own, other = m["kv"][...], m["kv_in"][l].astype(F32)
         first = jnp.where(even, own, other)
@@ -308,11 +327,16 @@
         prob = raised / jnp.sum(raised, axis=1, keepdims=True)
         rounded = prob.astype(BF16)
         att = dot_nn(rounded, v).astype(BF16)
+        m["k"][...], m["v"][...], m["att"][...] = k, v, att
+        m["rounded"][...] = rounded
+        m["factor"][...] = prob * (1.0 - squashed * squashed) * score_scale
+
+    def attention_backward(l):
+        k, v, q, att, ga = (m[n][...] for n in ("k", "v", "q", "att", "ga"))
         delta = jnp.sum(ga.astype(F32) * att.astype(F32), axis=1, keepdims=True)
-        ds = prob * (dot_nt(ga, v) - delta) * (1.0 - squashed * squashed) * score_scale
-        ds = ds.astype(BF16)
+        ds = (m["factor"][...] * (dot_nt(ga, v) - delta)).astype(BF16)
         dk_turned = dot_tn(ds, q)
-        dv = dot_tn(rounded, ga)
+        dv = dot_tn(m["rounded"][...], ga)
         dk = unrotate(dk_turned, cs[...], sn[...])
         lower = jnp.where(low, dk, pltpu.roll(dv, half, 1))
         upper = jnp.where(low, pltpu.roll(dk, half, 1), dv)
@@ -385,7 +409,10 @@
     for l in (1, 0):
         last = l == 0
         g, to = (m["g1"], g_out) if last else (m["g0"], m["g1"])
-        attention(l, g)
+        attention_upstream(l, g)
+        if not last:
+            attention_forward(1)
+        attention_backward(l)
         if not last:
             get_wo[0].start()
         normed = m["normed"]
@@ -430,10 +457,17 @@
                 v = v + dot_nn(m["dkv"][...], m["wkv"][:, at])
                 S[:, :, :, at] = v.astype(BF16).reshape(4, 2, RB, 384)
 
-            if k in (2, 1):
-                ring_b[k].start(0, 1, 2, 3)
-        ring_a[2].start(0, 1, 2, 3)
-        ring_a[1].start(0, 1, 2, 3)
+            if k == 2:
+                ring_b[2].start(0, 1, 2, 3)
+                ring_a[2].start(0, 1)
+                ring_a[1].start(0, 1)
+            elif k == 1:
+                ring_b[1].start(0, 1, 2, 3)
+                ring_a[2].start(2)
+                ring_a[1].start(2)
+            elif k == 3:
+                ring_a[2].start(3)
+                ring_a[1].start(3)
         if not last:
             for c in (*get_wkv[0], get_wq[0]):
                 c.start()
@@ -486,8 +520,12 @@
         both(lambda _, r2: r2.middle(1))
         aside(3)
         both(lambda r, r2: (r[0].finish(), r2.finish()))
-        to_x = remote(va.at[1 - xh], m["x_in"], m["s_x"].at[l], 0, **{XH: 1 - xh})
-        to_x.start()
+        to_x = [
+            remote(va.at[hh], m["x_in"].at[l, n], m["s_x"].at[l], n, **{XH: 1 - xh})
+            for n, hh in enumerate((1 - xh, xh))
+        ]
+        to_x[0].start()
+        to_x[1].start()
         if not last:
             front_kv(0)
 
@@ -506,15 +544,86 @@
             there = T[at, dp_cols(1 - xl)].astype(F32) + m["core_in"][l, 1 - xl, at, :].astype(F32)
             xl_out[at, :] = there.astype(BF16)
 
-        get_own[l].wait()
-        to_x.wait_recv()
-        rows = rows_of(z, xh)
-        grad = add(va.at[xh], m["x_in"])
-        rc = m["recip"][l, rows, :][:, :1]
-        gn = gain[l : l + 1, cols(y)]
-        unit = m["x_own"][l].astype(F32) * rc
-        u = grad * gn
-        per_feature = jnp.sum(grad * unit, axis=0, keepdims=True)
+        def norm_backward(n, hh):
+            get_own[l][n].wait()
+            to_x[n].wait_recv()
+            rows = rows_of(z, hh)
+            grad = add(va.at[hh], m["x_in"].at[l, n])
+            rc = m["recip"][l, rows, :][:, :1]
+            unit = m["x_own"][l, n].astype(F32) * rc
+            u = grad * gain[l : l + 1, cols(y)]
+            mean = m["stat"][rows, :][:, :1] * (1.0 / D)
+            upper = g[rows, cols(y)].astype(F32)
+            to[rows, cols(y)] = (upper + rc * (u - unit * mean)).astype(BF16)
+            return jnp.sum(grad * unit, axis=0, keepdims=True)
+
+        per_feature = norm_backward(0, xh)
+        def spread(zz, hh, yy, shift, width, n, dest):
+            ref = to.at[rows_of(zz, hh), cols(yy, width, shift)]
+            return remote(ref, ref, m["s_ag"].at[l], n, **dest)
+
+        def walk(first_axis, hh, base):
+            second = Y if first_axis == Z else Z
+            i, j = (z, y) if first_axis == Z else (y, z)
+            order = [i, lax.rem(i + 3, 4), lax.rem(i + 1, 4), lax.rem(i + 2, 4)]
+            up1, dn1 = {first_axis: lax.rem(i + 1, 4)}, {first_axis: lax.rem(i + 3, 4)}
+            up2, dn2 = {second: lax.rem(j + 1, 4)}, {second: lax.rem(j + 3, 4)}
+            jdn, jup, jfar = lax.rem(j + 3, 4), lax.rem(j + 1, 4), lax.rem(j + 2, 4)
+
+            def one(ii, jj, n, dest, shift=0, width=CB):
+                zz, yy = (ii, jj) if first_axis == Z else (jj, ii)
+                return spread(zz, hh, yy, shift, width, base + n, dest)
+
+            sent = []
+
+            def go(c):
+                c.start()
+                sent.append(c)
+
+            def begin():
+                go(one(order[0], j, 0, up1))
+                go(one(order[0], j, 1, dn1))
+                go(one(order[0], j, 4, up2))
+                go(one(order[0], j, 5, dn2))
+
+            def arrive_dn():
+                one(order[1], j, 0, up1).wait_recv()
+                go(one(order[1], j, 2, up1, 0, CA))
+
+            def arrive_up():
+                one(order[2], j, 1, dn1).wait_recv()
+                go(one(order[2], j, 3, dn1, CA, CB - CA))
+
+            def arrive_far():
+                one(order[3], j, 2, up1, 0, CA).wait_recv()
+                one(order[3], j, 3, dn1, CA, CB - CA).wait_recv()
+
+            def across(k):
+                go(one(order[k], j, 4 + 2 * k, up2))
+                go(one(order[k], j, 5 + 2 * k, dn2))
+
+            def second_step(k):
+                one(order[k], jdn, 4 + 2 * k, up2).wait_recv()
+                if k in (0, 2):
+                    go(one(order[k], jdn, 12 + k, up2))
+                one(order[k], jup, 5 + 2 * k, dn2).wait_recv()
+                if k in (1, 3):
+                    go(one(order[k], jup, 12 + k, dn2))
+
+            def last_step(k):
+                one(order[k], jfar, 12 + k, up2 if k in (0, 2) else dn2).wait_recv()
+
+            def done():
+                for c in sent:
+                    c.wait_send()
+
+            return begin, arrive_dn, arrive_up, arrive_far, second_step, last_step, done, across
+
+        own = walk(Z, xh, 0)
+        oth = walk(Y, 1 - xh, 16)
+        own[0]()
+        norm_backward(1, 1 - xh)
+        oth[0]()
         for n in range(9):
             k = n + 9 if last else n
             pack[k : k + 1, :] = per_feature[:, n * 128 : (n + 1) * 128]
@@ -525,79 +634,11 @@
             ]
             for c in to_g1:
                 c.start()
-        mean = m["stat"][rows, :][:, :1] * (1.0 / D)
-        up_own = g[rows, cols(y)].astype(F32)
-        to[rows, cols(y)] = (up_own + rc * (u - unit * mean)).astype(BF16)
-
-        def spread(zz, hh, yy, shift, width, n, dest):
-            ref = to.at[rows_of(zz, hh), cols(yy, width, shift)]
-            return remote(ref, ref, m["s_ag"].at[l], n, **dest)
-
-        def walk(first_axis, hh, base):
-            second = Y if first_axis == Z else Z
-            i, j = (z, y) if first_axis == Z else (y, z)
-            order = [i, lax.rem(i + 3, 4), lax.rem(i + 1, 4), lax.rem(i + 2, 4)]
-            up1, dn1 = {first_axis: lax.rem(i + 1, 4)}, {first_axis: lax.rem(i + 3, 4)}
-            up2, dn2 = {second: lax.rem(j + 1, 4)}, {second: lax.rem(j + 3, 4)}
-            jdn, jup, jfar = lax.rem(j + 3, 4), lax.rem(j + 1, 4), lax.rem(j + 2, 4)
-
-            def one(ii, jj, n, dest, shift=0, width=CB):
-                zz, yy = (ii, jj) if first_axis == Z else (jj, ii)
-                return spread(zz, hh, yy, shift, width, base + n, dest)
-
-            sent = []
-
-            def go(c):
-                c.start()
-                sent.append(c)
-
-            def begin():
-                go(one(order[0], j, 0, up1))
-                go(one(order[0], j, 1, dn1))
-                go(one(order[0], j, 4, up2))
-                go(one(order[0], j, 5, dn2))
-
-            def arrive_dn():
-                one(order[1], j, 0, up1).wait_recv()
-                go(one(order[1], j, 2, up1, 0, CA))
-
-            def arrive_up():
-                one(order[2], j, 1, dn1).wait_recv()
-                go(one(order[2], j, 3, dn1, CA, CB - CA))
-
-            def arrive_far():
-                one(order[3], j, 2, up1, 0, CA).wait_recv()
-                one(order[3], j, 3, dn1, CA, CB - CA).wait_recv()
-
-            def across(k):
-                go(one(order[k], j, 4 + 2 * k, up2))
-                go(one(order[k], j, 5 + 2 * k, dn2))
-
-            def second_step(k):
-                one(order[k], jdn, 4 + 2 * k, up2).wait_recv()
-                if k in (0, 2):
-                    go(one(order[k], jdn, 12 + k, up2))
-                one(order[k], jup, 5 + 2 * k, dn2).wait_recv()
-                if k in (1, 3):
-                    go(one(order[k], jup, 12 + k, dn2))
-
-            def last_step(k):
-                one(order[k], jfar, 12 + k, up2 if k in (0, 2) else dn2).wait_recv()
-
-            def done():
-                for c in sent:
-                    c.wait_send()
-
-            return begin, arrive_dn, arrive_up, arrive_far, second_step, last_step, done, across
-
-        mine = to.at[rows, cols(y)]
-        across = remote(mine, mine, m["s_ag_x"].at[l], 0, **{XH: 1 - xh})
-        across.start()
-        own = walk(Z, xh, 0)
-        oth = walk(Y, 1 - xh, 16)
-        own[0]()
         to_xl[l] = remote(xl_out, m["xl_in"].at[l], m["s_xl"].at[l], 0, **{XL: 1 - xl})
         to_xl[l].start()
+        own[1]()
+        own[7](1)
+        own[2]()
 
         @pl.loop(0, SEQ // 32)
         def _(r):
@@ -605,28 +646,22 @@
             here = T[at, dp_cols(xl)].astype(F32) + m["core_in"][l, xl, at, :].astype(F32)
             m["dw"][at, :] = here
 
-        own[1]()
-        own[7](1)
-        own[2]()
-        theirs = to.at[rows_of(z, 1 - xh), cols(y)]
-        remote(theirs, theirs, m["s_ag_x"].at[l], 0, **{XH: 1 - xh}).wait_recv()
-        oth[0]()
-        own[7](2)
-        if not last:
-            front_q(0)
         oth[1]()
         oth[7](1)
         oth[2]()
+        own[7](2)
         oth[7](2)
         own[3]()
         own[7](3)
-        own[4](0)
         oth[3]()
         oth[7](3)
+        own[4](0)
+        if not last:
+            front_q(0)
+        oth[4](0)
         own[4](1)
-        oth[4](0)
+        oth[4](1)
         own[4](2)
-        oth[4](1)
         if last:
             for c in to_g1:
                 c.wait_recv()
@@ -665,13 +700,15 @@
                     at = pl.ds(pl.multiple_of(yy * CB + k * 128, 128), 128)
                     gain_out[1:2, at] = ref[k : k + 1, :]
                     gain_out[0:1, at] = ref[9 + k : 10 + k, :]
+        if not last:
+            attention_forward(0)
         for k in range(4):
             own[5](k)
             oth[5](k)
 
         for r in (*ring_a.values(), *ring_b.values(), a2, b2):
             r.drain()
-        for c in (kv_pair[l], dkv_pair[l], to_x, across, *to_core, *stat_y[l], *stat_z[l], *stat_x[l]):
+        for c in (kv_pair[l], dkv_pair[l], *to_x, *to_core, *stat_y[l], *stat_z[l], *stat_x[l]):
             c.wait_send()
         own[6]()
         oth[6]()
@@ -696,12 +733,18 @@
         wkv=VMEM((HD, D), BF16),
         wq=VMEM((D, HD), BF16),
         wo=VMEM((HD, D), BF16),
-        x_own=VMEM((LAYERS, RB, CB), BF16),
+        x_own=VMEM((LAYERS, 2, RB, CB), BF16),
         recip=VMEM((LAYERS, SEQ, HD), F32),
         kv=VMEM((SEQ, HD), F32),
         kv_send=VMEM((LAYERS, SEQ, HD), BF16),
         kv_in=VMEM((LAYERS, SEQ, HD), BF16),
         q=VMEM((SEQ, HD), BF16),
+        k=VMEM((SEQ, HD), BF16),
+        v=VMEM((SEQ, HD), BF16),
+        att=VMEM((SEQ, HD), BF16),
+        ga=VMEM((SEQ, HD), BF16),
+        rounded=VMEM((SEQ, SEQ), BF16),
+        factor=VMEM((SEQ, SEQ), F32),
         keep=VMEM((SEQ, HD), BF16),
         send=VMEM((LAYERS, SEQ, HD), BF16),
         dkv_in=VMEM((LAYERS, SEQ, HD), BF16),
@@ -713,7 +756,7 @@
         ua=VMEM((4, RB, CB), BF16),
         ub=VMEM((4, RB, CB), BF16),
         va=VMEM((2, RB, CB), BF16),
-        x_in=VMEM((RB, CB), BF16),
+        x_in=VMEM((LAYERS, 2, RB, CB), BF16),
         squares=VMEM((SEQ, HD), F32),
         stat=VMEM((SEQ, HD), F32),
         stat_out=VMEM((LAYERS, 3, 8, SEQ), F32),
@@ -730,14 +773,13 @@
         s_kv=sem((LAYERS, 2, 1)),
         s_dkv=sem((LAYERS, 2, 1)),
         s_ring=sem((LAYERS, 10, 2, 6)),
-        s_x=sem((LAYERS, 2, 1)),
+        s_x=sem((LAYERS, 2, 2)),
         s_stat=sem((LAYERS, 2, 7)),
         s_core=sem((LAYERS, 2, 2)),
         s_xl=sem((LAYERS, 2, 1)),
         s_g1=sem((2, 7)),
         s_g2=sem((2, 3)),
         s_g3=sem((2, 3)),
-        s_ag_x=sem((LAYERS, 2, 1)),
         s_ag=sem((LAYERS, 2, 32)),
     )
     return pl.pallas_call(

time: 145 us -> 134 us (0.924)
  Pallas kernels: 144 us -> 133 us
    pallas_call x1, Pallas kernels: 141 us -> 130 us  [step(): pl.pallas_call(step_kernel, in_specs=[smem, smem, hbm, hbm, vmem, hbm, hb...]
where the time goes in v4:
time: 134 us
  Pallas kernels  133 us (99%)
    pallas_call x1, Pallas kernels, step(): pl.pallas_call(step_kernel, in_specs=[smem, smem, hbm, hbm, vmem, hbm, hb...  130 us
    pallas_call x1, Pallas kernels, write_out(): pl.pallas_call(write_kernel, in_specs=[pl.BlockSpec(memory_space=pltpu.VM...  2.93 us

profile of v4, /device:TPU:0, one launch (start us, length us, event | category | flops | bytes accessed | tf_op | source)
XLA Modules:
  0.0 134.0 jit_solution(7687179720040483265)
XLA Ops:
  0.6 130.3 %step.1 = (bf16[384,4608]{1,0:T(8,128)(2,1)S(1)}, f32[2,1152,128]{2,1,0:T(8,128)S(1)}, f32[2,64,1152]{2,1,0:T(8,128)S(1)}, f32[2,64,1152]{2,1,0:T(8,128)S(1)}, f...) custom-call(s32[1,4]{1,0:T(1,128)} %lengths.1, s32[2]{0:T(128)} %reach.1, bf16[2,384,4608]{2,1,0:T(8,128)(2,1)} %x_hbm.1, ...), custom_call_target="tpu_custom_call" | custom-call | tf_op jit(solution)/shard_map/step/pallas_call | solution.py:785
  130.9 2.9 %write_out.1 = (bf16[384,4608]{1,0:T(8,128)(2,1)}, f32[2,1152,128]{2,1,0:T(8,128)}, f32[2,64,1152]{2,1,0:T(8,128)}, f32[2,64,1152]{2,1,0:T(8,128)}, f32[2,128,1152]{2,1,0:T(8,128)}, /*index=5*/f32[2,4608]{1,0:T(2,128)}) custom-call(bf16[384,4608]{1,0:T(8,128)(2,1)S(1)} %get-tuple-element.18.refs_0_, f32[2,1152,128]{2,1,0:T(8,128)S(1)} %get-tuple-element.19.refs_1_, ...), custom_call_target="tpu_custom_call" | custom-call | tf_op jit(solution)/shard_map/write_out/pallas_call | solution.py:147

commit v5 on v4

--- a/solution.py
+++ b/solution.py
@@ -233,7 +233,14 @@
     for to in (*ymates, *zmates, *xmates):
         pl.semaphore_signal(barrier, inc=1, device_id=to, device_id_type=MESH)
 
-    kv_pair = [remote(m["kv_send"].at[l], m["kv_in"].at[l], m["s_kv"].at[l], 0, **pair) for l in (0, 1)]
+    halves = [pl.ds(0, SEQ // 2), pl.ds(SEQ // 2, SEQ // 2)]
+    kv_pair = [
+        [
+            remote(m["kv_send"].at[l, r], m["kv_in"].at[l, r], m["s_kv"].at[l], n, **pair)
+            for n, r in enumerate(halves)
+        ]
+        for l in (0, 1)
+    ]
     cs, sn = cosine, sine
 
     def front_norm(l, c):
@@ -257,21 +264,23 @@
         elif l == 1:
             get_x[0][c - 2].start()
 
-    def front_kv(l):
-        rc = jnp.sum(m["squares"][...], axis=1, keepdims=True) * (1.0 / D)
-        m["recip"][l] = jnp.broadcast_to(lax.rsqrt(rc + epsilon), (SEQ, HD))
-        for c in get_wkv[l]:
-            c.wait()
-        acc = jnp.zeros((SEQ, HD), F32)
+    def front_kv(l, n):
+        r = slice(n * SEQ // 2, (n + 1) * SEQ // 2)
+        rc = jnp.sum(m["squares"][r, :], axis=1, keepdims=True) * (1.0 / D)
+        m["recip"][l, r, :] = jnp.broadcast_to(lax.rsqrt(rc + epsilon), (SEQ // 2, HD))
+        if n == 0:
+            for c in get_wkv[l]:
+                c.wait()
+        acc = jnp.zeros((SEQ // 2, HD), F32)
         for c in range(3):
             at = slice(c * 1536, (c + 1) * 1536)
-            acc = acc + dot_nt(m["normed"][:, at], m["wkv"][:, at])
-        acc = acc * m["recip"][l]
-        m["kv"][...] = acc
-        m["kv_send"][l] = acc.astype(BF16)
-        if l == 1:
+            acc = acc + dot_nt(m["normed"][r, at], m["wkv"][:, at])
+        acc = acc * m["recip"][l, r, :]
+        m["kv"][r, :] = acc
+        m["kv_send"][l, r, :] = acc.astype(BF16)
+        if l == 1 and n == 0:
             pl.semaphore_wait(barrier, 13)
-        kv_pair[l].start()
+        kv_pair[l][n].start()
 
     def front_q(l):
         get_wq[l].wait()
@@ -294,7 +303,8 @@
         m["ga"][...] = ga.astype(BF16)
 
     def attention_forward(l):
-        kv_pair[l].wait_recv()
+        for c in kv_pair[l]:
+            c.wait_recv()
         own, other = m["kv"][...], m["kv_in"][l].astype(F32)
         first = jnp.where(even, own, other)
         second = jnp.where(even, other, own)
@@ -400,7 +410,8 @@
 
     for c in range(4):
         front_norm(1, c)
-    front_kv(1)
+        if c % 2:
+            front_kv(1, c // 2)
     front_q(1)
     pack = m["pack"]
     pack[...] = jnp.zeros((24, 128), F32)
@@ -425,10 +436,6 @@
         dkv_pair[l].wait_recv()
         dkv = add(m["keep"], m["dkv_in"].at[l])
         m["dkv"][...] = dkv.astype(BF16)
-        m["dqkv_t"][HD:] = (dkv * m["recip"][l]).astype(BF16).T
-        m["stat_out"][l, 1] = stat_sum(l, 0, stat_y[l])
-        for c in stat_z[l]:
-            c.start()
 
         ua, ub, va = m["ua"], m["ub"], m["va"]
         spans = ((0, CA), (CA, CB - CA), (0, CB))
@@ -472,6 +479,12 @@
             for c in (*get_wkv[0], get_wq[0]):
                 c.start()
 
+        dkv = add(m["keep"], m["dkv_in"].at[l])
+        m["dqkv_t"][HD:] = (dkv * m["recip"][l]).astype(BF16).T
+        m["stat_out"][l, 1] = stat_sum(l, 0, stat_y[l])
+        for c in stat_z[l]:
+            c.start()
+
         @pl.loop(0, D // 512)
         def _(c):
             at = pl.ds(pl.multiple_of(c * 512, 512), 512)
@@ -508,13 +521,13 @@
             to_xl[1].wait_recv()
         aside(0)
         both(lambda r, r2: (r[2].finish(), r2.start(0, 1)))
-        m["stat_out"][l, 2] = stat_sum(l, 1, stat_z[l])
-        stat_x[l][0].start()
         both(lambda r, _: r[3].middle(0, 1))
         aside(1)
         both(lambda r, r2: (r[1].finish(), r2.start(2)))
         both(lambda r, _: r[0].middle(0, 1))
         aside(2)
+        m["stat_out"][l, 2] = stat_sum(l, 1, stat_z[l])
+        stat_x[l][0].start()
         both(lambda r, r2: (r[3].finish(), r2.start(3)))
         both(lambda _, r2: r2.middle(0))
         both(lambda _, r2: r2.middle(1))
@@ -527,7 +540,8 @@
         to_x[0].start()
         to_x[1].start()
         if not last:
-            front_kv(0)
+            front_kv(0, 0)
+            front_kv(0, 1)
 
         total = stat_sum(l, 2, stat_x[l])
         m["stat"][...] = jnp.broadcast_to(total[:1], (HD, SEQ)).T
@@ -708,7 +722,7 @@
 
         for r in (*ring_a.values(), *ring_b.values(), a2, b2):
             r.drain()
-        for c in (kv_pair[l], dkv_pair[l], *to_x, *to_core, *stat_y[l], *stat_z[l], *stat_x[l]):
+        for c in (*kv_pair[l], dkv_pair[l], *to_x, *to_core, *stat_y[l], *stat_z[l], *stat_x[l]):
             c.wait_send()
         own[6]()
         oth[6]()
@@ -770,7 +784,7 @@
         gain_z=VMEM((4, 24, 128), F32),
         gain_y=VMEM((3, 24, 128), F32),
         s_local=sem((32,)),
-        s_kv=sem((LAYERS, 2, 1)),
+        s_kv=sem((LAYERS, 2, 2)),
         s_dkv=sem((LAYERS, 2, 1)),
         s_ring=sem((LAYERS, 10, 2, 6)),
         s_x=sem((LAYERS, 2, 2)),

time: 134 us -> 133 us (level)
  no operation moved by 1% of the time
where the time goes in v5:
time: 133 us
  Pallas kernels  132 us (99%)
    pallas_call x1, Pallas kernels, step(): pl.pallas_call(step_kernel, in_specs=[smem, smem, hbm, hbm, vmem, hbm, hb...  129 us
    pallas_call x1, Pallas kernels, write_out(): pl.pallas_call(write_kernel, in_specs=[pl.BlockSpec(memory_space=pltpu.VM...  2.93 us

profile of v5, /device:TPU:0, one launch (start us, length us, event | category | flops | bytes accessed | tf_op | source)
XLA Modules:
  0.0 132.7 jit_solution(11109551805118420372)
XLA Ops:
  0.6 129.0 %step.1 = (bf16[384,4608]{1,0:T(8,128)(2,1)S(1)}, f32[2,1152,128]{2,1,0:T(8,128)S(1)}, f32[2,64,1152]{2,1,0:T(8,128)S(1)}, f32[2,64,1152]{2,1,0:T(8,128)S(1)}, f...) custom-call(s32[1,4]{1,0:T(1,128)} %lengths.1, s32[2]{0:T(128)} %reach.1, bf16[2,384,4608]{2,1,0:T(8,128)(2,1)} %x_hbm.1, ...), custom_call_target="tpu_custom_call" | custom-call | tf_op jit(solution)/shard_map/step/pallas_call | solution.py:799
  129.7 2.9 %write_out.1 = (bf16[384,4608]{1,0:T(8,128)(2,1)}, f32[2,1152,128]{2,1,0:T(8,128)}, f32[2,64,1152]{2,1,0:T(8,128)}, f32[2,64,1152]{2,1,0:T(8,128)}, f32[2,128,1152]{2,1,0:T(8,128)}, /*index=5*/f32[2,4608]{1,0:T(2,128)}) custom-call(bf16[384,4608]{1,0:T(8,128)(2,1)S(1)} %get-tuple-element.18.refs_0_, f32[2,1152,128]{2,1,0:T(8,128)S(1)} %get-tuple-element.19.refs_1_, ...), custom_call_target="tpu_custom_call" | custom-call | tf_op jit(solution)/shard_map/write_out/pallas_call | solution.py:147
